TPU v7x, 256 devices: a whole 4x4x8 slice. The times are simulated.
256 devices in a mesh: pq: 8 (over z_hi, x), rs: 32 (over y, z_lo, core).
Axes of the slice: x: 4, y: 4, z: 8 (z_hi: 2, z_lo: 4; z = z_hi * 4 + z_lo), core: 2. Of those that a mesh axis runs over, the one named last changes fastest.
Arguments:
- integrals: bfloat16 [512, 1152, 1152], P('pq', 'rs'), may hold values from -6 to 6
- coeff: bfloat16 [1152, 896], P('rs', 'pq'), may hold values from -0.1875 to 0.1875
Outputs:
- half_mo: bfloat16 [512, 896, 896], P('pq', 'rs')
All inputs are finite; a program needn't handle non-finite values.
Results may differ from a plain program's by a relative error of at most 0.0049.
Values may be sent and summed in bfloat16 or wider, within the bound.
No kernel may reach another device: no remote copies, remote signals or barrier semaphores. Data moves between devices by JAX's collectives and lax.ppermute only.
A program may use at most 128 MiB of HBM per device.

v0:
```python
import jax
import jax.numpy as jnp
from jax import lax
from jax.sharding import PartitionSpec as P

NBASIS = 1152
NORB = 896


def joined_along(parts, dim):
    parts = jnp.moveaxis(parts, 0, dim)
    lengths = parts.shape
    return parts.reshape(*lengths[:dim], lengths[dim] * lengths[dim + 1], *lengths[dim + 2 :])


def from_everyone(array, axis):
    count = lax.axis_size(axis)
    return lax.all_to_all(
        jnp.broadcast_to(array[None], (count, *array.shape)), axis, 0, 0, tiled=True
    )


def collect(array, axis, dim):
    return joined_along(from_everyone(array, axis), dim)


def second_half(received, panel):
    return jnp.einsum("prl,rk->plk", received, panel, preferred_element_type=jnp.float32).astype(
        jnp.bfloat16
    )


def on_device(integrals, coeff):
    pair_rows = integrals.shape[0]
    block_rows = integrals.shape[1]
    flat = integrals.reshape(pair_rows * block_rows, NBASIS)
    strip = collect(coeff, "pq", 1)
    panel = collect(strip, "rs", 0)
    first = jnp.dot(flat, panel, preferred_element_type=jnp.float32).astype(jnp.bfloat16)
    first = first.reshape(pair_rows, block_rows, NORB)
    return second_half(lax.all_to_all(first, "rs", split_axis=2, concat_axis=1, tiled=True), panel)


def solution(mesh):
    placed = (P("pq", "rs", None), P("rs", "pq"))
    return jax.shard_map(
        on_device, mesh=mesh, in_specs=placed, out_specs=P("pq", "rs", None), check_vma=False
    )
```

profile of v0, /device:TPU:1, one launch (start us, length us, event | category | flops | bytes accessed | tf_op | source)
XLA Modules:
  0.0 255.1 jit_solution(5755505084666371884)
XLA Ops:
  0.0 0.7 broadcast_in_dim.6
  0.7 20.4 %all_to_all.25 = bf16[8,36,112]{2,1,0:T(8,128)(2,1)S(1)} all-to-all(bf16[8,36,112]{2,1,0:T(8,128)(2,1)S(1)} %broadcast_in_dim.6), channel_id=1, replica_groups=mesh['pq'=8,'rs'=32] {'pq'}, dimensions={0} | all-to-all | bytes 129024 | tf_op jit(solution)/shard_map/all_to_all | solution.py:18
  21.1 0.1 broadcast_in_dim.14
  21.3 1.6 broadcast_in_dim.15
  22.8 8.1 %all-to-all-start.1 = ((bf16[32,36,896]{2,1,0:T(8,128)(2,1)}), bf16[32,36,896]{2,1,0:T(8,128)(2,1)S(1)}, u32[]{:S(2)}, u32[]{:S(2)}) async-start(bf16[32,36,896]{2,1,0:T(8,128)(2,1)} %broadcast_in_dim.15), calls=%async_computation.1 | async-start | bytes 4587520 | tf_op jit(solution)/shard_map/all_to_all | solution.py:18
  30.9 8.0 %copy.15 = bf16[64,36,1152]{2,1,0:T(8,128)(2,1)} copy(bf16[64,36,1152]{2,0,1:T(8,128)(2,1)} %param.2) | data formatting | bytes 10616832 | tf_op args[0]
  39.0 8.9 %reshape.11 = bf16[2304,1152]{1,0:T(8,128)(2,1)} reshape(bf16[64,36,1152]{2,1,0:T(8,128)(2,1)} %copy.15) | data formatting | bytes 10616832 | tf_op jit(solution)/shard_map/reshape | solution.py:36
  47.8 37.1 %all-to-all-done.1 = bf16[32,36,896]{2,1,0:T(8,128)(2,1)S(1)} async-done(((bf16[32,36,896]{2,1,0:T(8,128)(2,1)}), bf16[32,36,896]{2,1,0:T(8,128)(2,1)S(1)}, u32[]{:S(2)}, u32[]{:S(2)}) %all-to-all-start.1) | async-done | bytes 2064416 | tf_op jit(solution)/shard_map/all_to_all | solution.py:18
  84.9 1.9 reshape.12
  86.9 10.0 %convolution_convert_fusion = bf16[2304,896]{1,0:T(8,128)(2,1)} fusion(bf16[2304,1152]{1,0:T(8,128)(2,1)} %reshape.11, bf16[1152,896]{1,0:T(8,128)(2,1)} %reshape.12), kind=kOutput, calls=%fused_computation.4 | convolution fusion | flops 4758405120 | bytes 11501568 | tf_op jit(solution)/shard_map/dot_general | solution.py:39
  96.8 6.9 %reshape.13 = bf16[64,36,896]{2,1,0:T(8,128)(2,1)} reshape(bf16[2304,896]{1,0:T(8,128)(2,1)} %convolution_convert_fusion) | data formatting | bytes 8257536 | tf_op jit(solution)/shard_map/reshape | solution.py:40
  103.7 13.9 %copy.17 = bf16[64,36,896]{0,1,2:T(8,128)(2,1)} copy(bf16[64,36,896]{2,1,0:T(8,128)(2,1)} %reshape.13) | data formatting | bytes 8257536 | tf_op jit(solution)/shard_map/reshape | solution.py:40
  117.6 13.7 %reshape.16 = bf16[32,2,32256]{2,1,0:T(2,128)(2,1)} reshape(bf16[896,36,64]{2,1,0:T(8,128)(2,1)} %bitcast.18) | data formatting | bytes 8257536
  131.3 99.3 %all_to_all.26 = bf16[32,2,32256]{2,1,0:T(2,128)(2,1)} all-to-all(bf16[32,2,32256]{2,1,0:T(2,128)(2,1)} %reshape.16), channel_id=1, replica_groups=mesh['pq'=8,'rs'=32] {'rs'}, dimensions={0} | all-to-all | bytes 8257536 | tf_op jit(solution)/shard_map/all_to_all | solution.py:41
  230.6 14.6 %reshape.17 = bf16[896,36,64]{2,1,0:T(8,128)(2,1)} reshape(bf16[32,2,32256]{2,1,0:T(2,128)(2,1)} %all_to_all.26) | data formatting | bytes 8257536
  245.2 9.9 %bitcast_convert_fusion = bf16[64,28,896]{2,0,1:T(8,128)(2,1)} fusion(bf16[64,36,32,28]{0,1,3,2:T(8,128)(2,1)} %bitcast.17, bf16[32,36,896]{2,1,0:T(8,128)(2,1)S(1)} %all-to-all-done.1), kind=kOutput, calls=%fused_computation.3 | convolution fusion | flops 3700981760 | bytes 9404416 | tf_op jit(solution)/shard_map/prl,rk->plk/dot_general | solution.py:28
  (1 shorter events, 0.0 us)
Async XLA Ops:
  22.8 62.1 %all-to-all-start.1 = ((bf16[32,36,896]{2,1,0:T(8,128)(2,1)}), bf16[32,36,896]{2,1,0:T(8,128)(2,1)S(1)}, u32[]{:S(2)}, u32[]{:S(2)}) async-start(bf16[32,36,896]{2,1,0:T(8,128)(2,1)} %broadcast_in_dim.15), calls=%async_computation.1 | async-start | bytes 4587520 | tf_op jit(solution)/shard_map/all_to_all | solution.py:18
where the time goes:
time: 257 us; the launch traced here: 255 us
  blocking collectives  120 us (47%)
  local copies, waits for them, and re-layouts  70.4 us (27%)
  waiting for transfers between devices  37.1 us (14%)
  matrix products  19.8 us (8%)
  starting transfers between devices  8.09 us (3%)
    all_to_all x1, blocking collectives, on_device(): lax.all_to_all(first, 'rs', split_axis=2, concat_axis=1, tiled=True)  99.3 us
    all_to_all x1, waiting for transfers between devices, from_everyone(): lax.all_to_all(jnp.broadcast_to(array[None], (count, *array.shape)), axis...  37.1 us
    unnamed x3, local copies, waits for them, and re-layouts  36.4 us
    reshape x2, local copies, waits for them, and re-layouts, on_device(): first = first.reshape(pair_rows, block_rows, NORB)  20.8 us
    all_to_all x1, blocking collectives, from_everyone(): lax.all_to_all(jnp.broadcast_to(array[None], (count, *array.shape)), axis...  20.4 us
    dot_general x1, matrix products, on_device(): jnp.dot(flat, panel, preferred_element_type=jnp.float32)  9.95 us
    dot_general x1, matrix products, second_half(): jnp.einsum('prl,rk->plk', received, panel, preferred_element_type=jnp.flo...  9.88 us
    reshape x1, local copies, waits for them, and re-layouts, on_device(): flat = integrals.reshape(pair_rows * block_rows, NBASIS)  8.88 us
  transfers between devices with their start and end apart: 1, of which 1 were waited for; matrix products, arithmetic and copies ran while one was open for 7% of the time, Pallas kernels for 0%

commit v1 on v0

v1 whole, which is shorter than its diff:
```python
import jax
import jax.numpy as jnp
from jax import lax
from jax.experimental import pallas as pl
from jax.experimental.pallas import tpu as pltpu
from jax.sharding import PartitionSpec as P


NBASIS = 1152
NORB = 896
SIZES = (8, 16, 4)
BOTH = ("pq", "rs")


def place(z_hi, x, y, z_lo, core):
    return (z_hi * 4 + x) * 32 + y * 8 + z_lo * 2 + core


ALONG_Z = [
    [place(h, x, y, z, c) for h in range(2) for z in range(4) for c in range(2)]
    for x in range(4)
    for y in range(4)
]
ACROSS = [
    [place(h, x, y, z, c) for x in range(4) for y in range(4)]
    for h in range(2)
    for z in range(4)
    for c in range(2)
]


def from_group(array, groups):
    copies = jnp.broadcast_to(array[None], (len(groups[0]), *array.shape))
    return lax.all_to_all(copies, BOTH, 0, 0, tiled=True, axis_index_groups=groups)


def one_hot(match):
    return match.astype(jnp.bfloat16)


def pick(array, chosen):
    return jnp.dot(array, chosen, preferred_element_type=jnp.float32).astype(jnp.bfloat16)


def join_kernel(own_ref, a_ref, b_ref, c_ref, d_ref, out_ref, *, width):
    total = jnp.zeros(out_ref.shape, jnp.float32)
    for step, ref in enumerate((a_ref, b_ref, c_ref, d_ref)):
        for h in range(2):
            owner = h * 4 + (own_ref[0] ^ step)
            inside = lax.broadcasted_iota(jnp.int32, (128, NORB), 0)
            column = lax.broadcasted_iota(jnp.int32, (128, NORB), 1)
            keep = (inside < width) & (column == owner * width + inside)
            chosen = jnp.where(keep, 1.0, 0.0).astype(jnp.bfloat16)
            total += jnp.dot(ref[h], chosen, preferred_element_type=jnp.float32)
    out_ref[...] = total.astype(out_ref.dtype)


def join(slabs, x, width):
    block = 384
    return pl.pallas_call(
        lambda *refs: join_kernel(*refs, width=width),
        grid=(NBASIS // block,),
        in_specs=[pl.BlockSpec(memory_space=pltpu.SMEM)]
        + [pl.BlockSpec((2, block, 128), lambda i: (0, i, 0))] * 4,
        out_specs=pl.BlockSpec((block, NORB), lambda i: (i, 0)),
        out_shape=jax.ShapeDtypeStruct((NBASIS, NORB), jnp.bfloat16),
        name="join",
    )(x.reshape(1), *slabs)


def leave(part, flat, count, lanes):
    first = jnp.einsum("sc,ms->cm", part, flat, preferred_element_type=jnp.float32)
    return first.astype(jnp.bfloat16).reshape(count, -1, lanes)


def on_device(integrals, coeff):
    pairs, rows, _ = integrals.shape
    width = coeff.shape[1]
    count = lax.axis_size("rs")
    mine = NORB // count
    x = lax.axis_index("pq") % 4
    y = lax.axis_index("rs") // 8
    flat = integrals.transpose(1, 0, 2).reshape(rows * pairs, NBASIS)

    strip = from_group(jnp.pad(coeff, ((0, 0), (0, 128 - width))), ALONG_Z)
    strip = strip.reshape(2, 8 * rows, 128)

    size = SIZES[0]
    inner, outer = lax.broadcasted_iota(jnp.int32, (128, 4 * size), 0), lax.broadcasted_iota(
        jnp.int32, (128, 4 * size), 1
    )
    chosen = one_hot(inner == outer // size * mine + outer % size)
    early = pick(strip.reshape(16 * rows, 128), chosen)
    early_sent = early.reshape(-1, 8, 128)
    early = from_group(early_sent, ACROSS)
    early = early.reshape(4, 4, 2, 8 * rows, 4 * size).transpose(1, 3, 2, 0, 4)
    early = early.reshape(NBASIS, count * size)

    first = leave(early, flat, count, rows * pairs)

    strip, _ = lax.optimization_barrier((strip, early_sent))
    stack = [strip]
    for step in (1, 2, 3):
        stack.append(
            lax.ppermute(strip, "rs", [(j, (j // 8 ^ step) * 8 + j % 8) for j in range(32)])
        )
    low, high = y % 2 == 1, y // 2 == 1
    stack = [jnp.where(low, stack[i ^ 1], stack[i]) for i in range(4)]
    stack = jnp.stack([jnp.where(high, stack[i ^ 2], stack[i]) for i in range(4)], 1)
    slabs = [stack.reshape(2, NBASIS, 128)]
    for step in (1, 2, 3):
        slabs.append(lax.ppermute(slabs[0], "pq", [(i, i & 4 | (i & 3) ^ step) for i in range(8)]))
    panel = join(slabs, x, width)
    by_row = panel.reshape(count, rows, NORB)

    outs = []
    lo = 0
    for size in SIZES:
        if lo:
            target = lax.broadcasted_iota(jnp.int32, (NORB, count * size), 1)
            source = lax.broadcasted_iota(jnp.int32, (NORB, count * size), 0)
            part = pick(panel, one_hot(source == target // size * mine + lo + target % size))
            part, _ = lax.optimization_barrier((part, first))
            first = leave(part, flat, count, rows * pairs)
        lo += size
        got = lax.all_to_all(first, "rs", 0, 0, tiled=True)
        got = got.reshape(count, size, rows, pairs)
        outs.append(
            jnp.einsum("jlrp,jrk->lpk", got, by_row, preferred_element_type=jnp.float32).astype(
                jnp.bfloat16
            )
        )
    return jnp.concatenate(outs, 0).transpose(1, 0, 2)


def solution(mesh):
    placed = (P("pq", "rs", None), P("rs", "pq"))
    return jax.shard_map(
        on_device, mesh=mesh, in_specs=placed, out_specs=P("pq", "rs", None), check_vma=False
    )
```

time: 257 us -> 221 us (0.86)
  blocking collectives: 120 us -> 59.7 us
  local copies, waits for them, and re-layouts: 70.4 us -> 22.6 us
  waiting for transfers between devices: 37.1 us -> 72.3 us
  starting transfers between devices: 8.09 us -> 28.6 us
  matrix products: 19.8 us -> 27.6 us
  Pallas kernels: 0 us -> 6.96 us
    all_to_all x2, blocking collectives: 120 us -> 59.7 us  [on_device(): got = lax.all_to_all(first, 'rs', 0, 0, tiled=True)]
    unnamed x3 -> x12, local copies, waits for them, and re-layouts: 36.4 us -> 0.02 us
    all_to_all x1 -> x3, waiting for transfers between devices: 37.1 us -> 55.3 us  [the longest x1 41 us: on_device(): got = lax.all_to_all(first, 'rs', 0, 0, tiled=True)]
    ppermute x0 -> x6, waiting for transfers between devices: none -> 17 us  [the longest x3 15.3 us: on_device(): lax.ppermute(slabs[0], 'pq', [(i, i & 4 | i & 3 ^ step) for i in range(8)])]
    reshape x4 -> x8, local copies, waits for them, and re-layouts: 31.6 us -> 17.4 us  [the longest x3 13.2 us: on_device(): got = got.reshape(count, size, rows, pairs)]
    all_to_all x1 -> x3, starting transfers between devices: 8.09 us -> 21.3 us  [the longest x2 16.5 us: from_group(): lax.all_to_all(copies, BOTH, 0, 0, tiled=True, axis_index_groups=groups)]
    dot_general x2 -> x9, matrix products: 19.8 us -> 27.6 us  [the longest x3 12.1 us: on_device(): jnp.einsum('jlrp,jrk->lpk', got, by_row, preferred_element_type=jnp.float32)]
    ppermute x0 -> x6, starting transfers between devices: none -> 7.26 us  [the longest x3 4.01 us: on_device(): lax.ppermute(strip, 'rs', [(j, (j // 8 ^ step) * 8 + j % 8) for j in rang...]
  transfers between devices with their start and end apart: 1 -> 9, of which waited for: 1 -> 5; matrix products, arithmetic and copies ran while one was open for 7% -> 11% of each run, Pallas kernels for 0% -> 0%
where the time goes in v1:
time: 221 us; the launch traced here: 220 us
  waiting for transfers between devices  72.3 us (33%)
  blocking collectives  59.7 us (27%)
  starting transfers between devices  28.6 us (13%)
  matrix products  27.6 us (12%)
  local copies, waits for them, and re-layouts  22.6 us (10%)
  Pallas kernels  6.96 us (3%)
    all_to_all x2, blocking collectives, on_device(): got = lax.all_to_all(first, 'rs', 0, 0, tiled=True)  59.7 us
    all_to_all x1, waiting for transfers between devices, on_device(): got = lax.all_to_all(first, 'rs', 0, 0, tiled=True)  41 us
    all_to_all x2, starting transfers between devices, from_group(): lax.all_to_all(copies, BOTH, 0, 0, tiled=True, axis_index_groups=groups)  16.5 us
    ppermute x3, waiting for transfers between devices, on_device(): lax.ppermute(slabs[0], 'pq', [(i, i & 4 | i & 3 ^ step) for i in range(8)])  15.3 us
    all_to_all x2, waiting for transfers between devices, from_group(): lax.all_to_all(copies, BOTH, 0, 0, tiled=True, axis_index_groups=groups)  14.3 us
    reshape x3, local copies, waits for them, and re-layouts, on_device(): got = got.reshape(count, size, rows, pairs)  13.2 us
    dot_general x3, matrix products, on_device(): jnp.einsum('jlrp,jrk->lpk', got, by_row, preferred_element_type=jnp.float32)  12.1 us
    dot_general x3, matrix products, leave(): jnp.einsum('sc,ms->cm', part, flat, preferred_element_type=jnp.float32)  11.5 us
  transfers between devices with their start and end apart: 9, of which 5 were waited for; matrix products, arithmetic and copies ran while one was open for 11% of the time, Pallas kernels for 0%

profile of v1, /device:TPU:1, one launch (start us, length us, event | category | flops | bytes accessed | tf_op | source)
XLA Modules:
  0.0 220.2 jit_solution(4957077509381381082)
XLA Ops:
  1.4 10.0 %all-to-all-start = ((bf16[16,36,128]{2,1,0:T(8,128)(2,1)}), bf16[16,36,128]{2,1,0:T(8,128)(2,1)S(1)}, u32[]{:S(2)}, u32[]{:S(2)}) async-start(bf16[16,36,128]{2,1,0:T(8,128)(2,1)} %broadcast_in_dim.6), calls=%async_computation | async-start | bytes 327680 | tf_op jit(solution)/shard_map/all_to_all | solution.py:34
  11.5 9.4 %all-to-all-done = bf16[16,36,128]{2,1,0:T(8,128)(2,1)S(1)} async-done(((bf16[16,36,128]{2,1,0:T(8,128)(2,1)}), bf16[16,36,128]{2,1,0:T(8,128)(2,1)S(1)}, u32[]{:S(2)}, u32[]{:S(2)}) %all-to-all-start) | async-done | bytes 147488 | tf_op jit(solution)/shard_map/all_to_all | solution.py:34
  22.3 2.6 %collective-permute-start.1 = (bf16[2,288,128]{2,1,0:T(8,128)(2,1)S(1)}, bf16[2,288,128]{2,1,0:T(8,128)(2,1)S(1)}, u32[]{:S(2)}, u32[]{:S(2)}) collective-permute-start(bf16[2,288,128]{2,1,0:T(8,128)(2,1)S(1)} %reshape.48), channel_id=1, source_target_pairs={{0,16},{1,17},{2,18},{3,19},{4,20},{5,21},{6,22},{7,23},{8,24},{9,... | collective-permute-start | bytes 442376 | tf_op jit(solution)/shard_map/ppermute | solution.py:105
  26.4 6.5 %all-to-all-start.1 = ((bf16[16,18,8,128]{3,2,1,0:T(8,128)(2,1)}), bf16[16,18,8,128]{3,2,1,0:T(8,128)(2,1)S(1)}, u32[]{:S(2)}, u32[]{:S(2)}) async-start(bf16[16,18,8,128]{3,2,1,0:T(8,128)(2,1)} %broadcast_in_dim.15), calls=%async_computation.1 | async-start | bytes 1179648 | tf_op jit(solution)/shard_map/all_to_all | solution.py:34
  35.6 2.5 %collective-permute-start.5 = (bf16[2,1152,128]{2,1,0:T(8,128)(2,1)}, bf16[2,1152,128]{2,1,0:T(8,128)(2,1)}, u32[]{:S(2)}, u32[]{:S(2)}) collective-permute-start(bf16[2,1152,128]{2,1,0:T(8,128)(2,1)} %bitcast.9.refs_1_), channel_id=1, source_target_pairs={{0,96},{32,64},{64,32},{96,0},{128,224},{160,192},{192,160},{224,1... | collective-permute-start | bytes 1769480 | tf_op jit(solution)/shard_map/ppermute | solution.py:112
  38.9 4.9 %all-to-all-done.1 = bf16[16,18,8,128]{3,2,1,0:T(8,128)(2,1)S(1)} async-done(((bf16[16,18,8,128]{3,2,1,0:T(8,128)(2,1)}), bf16[16,18,8,128]{3,2,1,0:T(8,128)(2,1)S(1)}, u32[]{:S(2)}, u32[]{:S(2)}) %all-to-all-start.1) | async-done | bytes 589856 | tf_op jit(solution)/shard_map/all_to_all | solution.py:34
  44.7 1.7 copy.16
  47.0 5.3 %fusion = bf16[32,8,2304]{2,1,0:T(8,128)(2,1)} fusion(bf16[1152,256]{0,1:T(8,128)(2,1)S(1)} %reshape.43, bf16[2304,1152]{1,0:T(8,128)(2,1)} %bitcast.57), kind=kOutput, calls=%fused_computation.2 | convolution fusion | flops 1359544320 | bytes 7077888 | tf_op jit(solution)/shard_map/sc,ms->cm/dot_general | solution.py:72
  52.3 15.2 %collective-permute-done.5.refs_4_ = bf16[2,1152,128]{2,1,0:T(8,128)(2,1)} collective-permute-done((bf16[2,1152,128]{2,1,0:T(8,128)(2,1)}, bf16[2,1152,128]{2,1,0:T(8,128)(2,1)}, u32[]{:S(2)}, u32[]{:S(2)}) %collective-permute-start.5) | collective-permute-done | bytes 589856 | tf_op jit(solution)/shard_map/ppermute | solution.py:112
  67.5 7.0 %join.1 = bf16[1152,896]{1,0:T(8,128)(2,1)} custom-call(s32[1]{0:T(128)} %bitcast.4.refs_0_, bf16[2,1152,128]{2,1,0:T(8,128)(2,1)} %bitcast.9.refs_1_, bf16[2,1152,128]{2,1,0:T(8,128)(2,1)} %collective-permute-done.3.refs_2_, bf16[2,1152,128]{2,1,0:T(8,128)(2,1)} %collective-permute-done.4.refs_3_, bf16[2,1152,128]{2,1,0:T(8,128)(2,1)} %collective-permute-done.5.refs_4_), custom_call_target="tpu_custom_call" | custom-call | tf_op jit(solution)/shard_map/join/pallas_call | solution.py:60
  74.5 3.2 %convolution_convert_fusion.3 = bf16[1152,512]{1,0:T(8,128)(2,1)S(1)} fusion(bf16[1152,896]{1,0:T(8,128)(2,1)} %join.1, s32[512]{0:T(512)S(1)} %get-tuple-element.20, s32[512]{0:T(512)S(1)} %get-tuple-element.21, s32[512]{0:T(512)S(1)} %get-tuple-element.19, s32[512]{0:T(512)S(1)} %get-tuple-element.22, pred[512]{0:T(512)(128)(4,1)S(1)} %get-tuple-element.24, ...), kind=kOutput, calls=%fused_computation.6 | convolution fusion | flops 1060306944 | bytes 3253248 | tf_op jit(solution)/shard_map/dot_general | solution.py:42
  77.7 4.6 %convolution_convert_fusion = bf16[512,2304]{1,0:T(8,128)(2,1)} fusion(bf16[1152,512]{1,0:T(8,128)(2,1)S(1)} %convolution_convert_fusion.3, bf16[2304,1152]{1,0:T(8,128)(2,1)S(1)} %bitcast.60), kind=kOutput, calls=%fused_computation | convolution fusion | flops 2719088640 | bytes 8847360 | tf_op jit(solution)/shard_map/sc,ms->cm/dot_general | solution.py:72
  84.8 24.3 %all_to_all.25 = bf16[32,4,2304]{2,1,0:T(4,128)(2,1)S(1)} all-to-all(bf16[32,4,2304]{2,1,0:T(4,128)(2,1)S(1)} %reshape.53), channel_id=1, replica_groups=mesh['pq'=8,'rs'=32] {'rs'}, dimensions={0} | all-to-all | bytes 1179648 | tf_op jit(solution)/shard_map/all_to_all | solution.py:126
  109.1 35.4 %all_to_all.26 = bf16[32,8,2304]{2,1,0:T(8,128)(2,1)} all-to-all(bf16[32,8,2304]{2,1,0:T(8,128)(2,1)} %fusion), channel_id=1, replica_groups=mesh['pq'=8,'rs'=32] {'rs'}, dimensions={0} | all-to-all | bytes 2359296 | tf_op jit(solution)/shard_map/all_to_all | solution.py:126
  144.5 4.8 %all-to-all-start.3 = ((bf16[32,16,2304]{2,1,0:T(8,128)(2,1)}), bf16[32,16,2304]{2,1,0:T(8,128)(2,1)}, u32[]{:S(2)}, u32[]{:S(2)}) async-start(bf16[32,16,2304]{2,1,0:T(8,128)(2,1)} %bitcast.62), calls=%async_computation.3 | async-start | bytes 4718592 | tf_op jit(solution)/shard_map/all_to_all | solution.py:126
  149.3 2.5 %reshape.55 = bf16[32,36,896,1]{2,1,0,3:T(8,128)(2,1)S(1)} reshape(bf16[1152,896]{1,0:T(8,128)(2,1)} %join.1) | data formatting | bytes 4128768 | tf_op jit(solution)/shard_map/reshape | solution.py:114
  151.9 2.0 reshape.54
  153.9 3.0 %fusion.9 = bf16[4,64,896]{2,1,0:T(8,128)(2,1)} fusion(bf16[32,4,36,64]{3,2,0,1:T(8,128)(2,1)} %reshape.54, bf16[32,36,896,1]{2,1,0,3:T(8,128)(2,1)S(1)} %reshape.55), kind=kOutput, calls=%fused_computation.15 | convolution fusion | flops 528711680 | bytes 3112960 | tf_op jit(solution)/shard_map/jlrp,jrk->lpk/dot_general | solution.py:129
  156.9 3.4 %reshape.46 = bf16[32,8,36,64]{3,2,1,0:T(8,128)(2,1)S(1)} reshape(bf16[32,8,2304]{2,1,0:T(8,128)(2,1)} %all_to_all.26) | data formatting | bytes 2359296 | tf_op jit(solution)/shard_map/reshape | solution.py:127
  160.3 3.3 %bitcast_convert_fusion.1 = bf16[8,64,896]{2,1,0:T(8,128)(2,1)S(1)} fusion(bf16[32,8,36,64]{3,2,1,0:T(8,128)(2,1)S(1)} %reshape.46, bf16[32,36,896,1]{2,1,0,3:T(8,128)(2,1)} %copy-done), kind=kOutput, calls=%fused_computation.12 | convolution fusion | flops 1057423360 | bytes 4161536 | tf_op jit(solution)/shard_map/jlrp,jrk->lpk/dot_general | solution.py:129
  163.7 41.0 %all-to-all-done.3 = bf16[32,16,2304]{2,1,0:T(8,128)(2,1)} async-done(((bf16[32,16,2304]{2,1,0:T(8,128)(2,1)}), bf16[32,16,2304]{2,1,0:T(8,128)(2,1)}, u32[]{:S(2)}, u32[]{:S(2)}) %all-to-all-start.3) | async-done | bytes 2359328 | tf_op jit(solution)/shard_map/all_to_all | solution.py:126
  204.7 7.8 %reshape.52 = bf16[32,16,36,64]{3,2,1,0:T(8,128)(2,1)} reshape(bf16[32,16,2304]{2,1,0:T(8,128)(2,1)} %all-to-all-done.3) | data formatting | bytes 4718592 | tf_op jit(solution)/shard_map/reshape | solution.py:127
  212.5 5.7 %bitcast_convert_fusion = bf16[16,64,896]{2,1,0:T(8,128)(2,1)S(1)} fusion(bf16[32,16,36,64]{3,2,1,0:T(8,128)(2,1)} %reshape.52, bf16[32,36,896,1]{2,1,0,3:T(8,128)(2,1)S(1)} %copy-done.1), kind=kOutput, calls=%fused_computation.3 | convolution fusion | flops 2114846720 | bytes 6258688 | tf_op jit(solution)/shard_map/jlrp,jrk->lpk/dot_general | solution.py:129
  218.3 1.9 maximum_bitcast_fusion
  (48 shorter events, 11.7 us)
Async XLA Ops:
  1.4 19.5 %all-to-all-start = ((bf16[16,36,128]{2,1,0:T(8,128)(2,1)}), bf16[16,36,128]{2,1,0:T(8,128)(2,1)S(1)}, u32[]{:S(2)}, u32[]{:S(2)}) async-start(bf16[16,36,128]{2,1,0:T(8,128)(2,1)} %broadcast_in_dim.6), calls=%async_computation | async-start | bytes 327680 | tf_op jit(solution)/shard_map/all_to_all | solution.py:34
  20.9 12.0 %collective-permute-start.2 = (bf16[2,288,128]{2,1,0:T(8,128)(2,1)S(1)}, bf16[2,288,128]{2,1,0:T(8,128)(2,1)S(1)}, u32[]{:S(2)}, u32[]{:S(2)}) collective-permute-start(bf16[2,288,128]{2,1,0:T(8,128)(2,1)S(1)} %reshape.48), channel_id=1, source_target_pairs={{0,8},{1,9},{2,10},{3,11},{4,12},{5,13},{6,14},{7,15},{8,0},{9,1},... | collective-permute-start | bytes 442376 | tf_op jit(solution)/shard_map/ppermute | solution.py:105
  22.3 10.6 %collective-permute-start.1 = (bf16[2,288,128]{2,1,0:T(8,128)(2,1)S(1)}, bf16[2,288,128]{2,1,0:T(8,128)(2,1)S(1)}, u32[]{:S(2)}, u32[]{:S(2)}) collective-permute-start(bf16[2,288,128]{2,1,0:T(8,128)(2,1)S(1)} %reshape.48), channel_id=1, source_target_pairs={{0,16},{1,17},{2,18},{3,19},{4,20},{5,21},{6,22},{7,23},{8,24},{9,... | collective-permute-start | bytes 442376 | tf_op jit(solution)/shard_map/ppermute | solution.py:105
  24.9 9.7 %collective-permute-start = (bf16[2,288,128]{2,1,0:T(8,128)(2,1)S(1)}, bf16[2,288,128]{2,1,0:T(8,128)(2,1)S(1)}, u32[]{:S(2)}, u32[]{:S(2)}) collective-permute-start(bf16[2,288,128]{2,1,0:T(8,128)(2,1)S(1)} %reshape.48), channel_id=1, source_target_pairs={{0,24},{1,25},{2,26},{3,27},{4,28},{5,29},{6,30},{7,31},{8,16},{9,... | collective-permute-start | bytes 442376 | tf_op jit(solution)/shard_map/ppermute | solution.py:105
  26.4 17.4 %all-to-all-start.1 = ((bf16[16,18,8,128]{3,2,1,0:T(8,128)(2,1)}), bf16[16,18,8,128]{3,2,1,0:T(8,128)(2,1)S(1)}, u32[]{:S(2)}, u32[]{:S(2)}) async-start(bf16[16,18,8,128]{3,2,1,0:T(8,128)(2,1)} %broadcast_in_dim.15), calls=%async_computation.1 | async-start | bytes 1179648 | tf_op jit(solution)/shard_map/all_to_all | solution.py:34
  35.6 31.9 %collective-permute-start.5 = (bf16[2,1152,128]{2,1,0:T(8,128)(2,1)}, bf16[2,1152,128]{2,1,0:T(8,128)(2,1)}, u32[]{:S(2)}, u32[]{:S(2)}) collective-permute-start(bf16[2,1152,128]{2,1,0:T(8,128)(2,1)} %bitcast.9.refs_1_), channel_id=1, source_target_pairs={{0,96},{32,64},{64,32},{96,0},{128,224},{160,192},{192,160},{224,1... | collective-permute-start | bytes 1769480 | tf_op jit(solution)/shard_map/ppermute | solution.py:112
  38.1 29.4 %collective-permute-start.4 = (bf16[2,1152,128]{2,1,0:T(8,128)(2,1)}, bf16[2,1152,128]{2,1,0:T(8,128)(2,1)}, u32[]{:S(2)}, u32[]{:S(2)}) collective-permute-start(bf16[2,1152,128]{2,1,0:T(8,128)(2,1)} %bitcast.9.refs_1_), channel_id=1, source_target_pairs={{0,64},{32,96},{64,0},{96,32},{128,192},{160,224},{192,128},{224,1... | collective-permute-start | bytes 1769480 | tf_op jit(solution)/shard_map/ppermute | solution.py:112
  38.6 28.9 %collective-permute-start.3 = (bf16[2,1152,128]{2,1,0:T(8,128)(2,1)}, bf16[2,1152,128]{2,1,0:T(8,128)(2,1)}, u32[]{:S(2)}, u32[]{:S(2)}) collective-permute-start(bf16[2,1152,128]{2,1,0:T(8,128)(2,1)} %bitcast.9.refs_1_), channel_id=1, source_target_pairs={{0,32},{32,0},{64,96},{96,64},{128,160},{160,128},{192,224},{224,1... | collective-permute-start | bytes 1769480 | tf_op jit(solution)/shard_map/ppermute | solution.py:112
  67.5 10.2 %slice-start = ((s8[5308416]{0:T(1024)(128)(4,1)}), s8[1114112]{0:T(1024)(128)(4,1)S(1)}, s32[]{:S(2)}) async-start(s8[5308416]{0:T(1024)(128)(4,1)} %bitcast.58), calls=%async_computation.5 | async-start | bytes 2228224
  74.5 3.2 %slice-start.1 = ((s8[5308416]{0:T(1024)(128)(4,1)}), s8[4194304]{0:T(1024)(128)(4,1)S(1)}, s32[]{:S(2)}) async-start(s8[5308416]{0:T(1024)(128)(4,1)} %bitcast.58), calls=%async_computation.6 | async-start | bytes 8388608
  77.7 4.7 %copy-start.2 = (bf16[1152,896]{1,0:T(8,128)(2,1)S(1)}, bf16[1152,896]{1,0:T(8,128)(2,1)}, u32[]{:S(2)}) copy-start(bf16[1152,896]{1,0:T(8,128)(2,1)} %join.1) | copy-start | bytes 6193156
  144.5 60.2 %all-to-all-start.3 = ((bf16[32,16,2304]{2,1,0:T(8,128)(2,1)}), bf16[32,16,2304]{2,1,0:T(8,128)(2,1)}, u32[]{:S(2)}, u32[]{:S(2)}) async-start(bf16[32,16,2304]{2,1,0:T(8,128)(2,1)} %bitcast.62), calls=%async_computation.3 | async-start | bytes 4718592 | tf_op jit(solution)/shard_map/all_to_all | solution.py:126
  151.8 2.1 copy-start
  163.7 48.9 %copy-start.1 = (bf16[32,36,896,1]{2,1,0,3:T(8,128)(2,1)S(1)}, bf16[32,36,896,1]{2,1,0,3:T(8,128)(2,1)}, u32[]{:S(2)}) copy-start(bf16[32,36,896,1]{2,1,0,3:T(8,128)(2,1)} %copy-done) | copy-start | bytes 6193156
  212.5 5.7 %copy-start.3 = (bf16[4,64,896]{2,1,0:T(8,128)(2,1)S(1)}, bf16[4,64,896]{2,1,0:T(8,128)(2,1)}, u32[]{:S(2)}) copy-start(bf16[4,64,896]{2,1,0:T(8,128)(2,1)} %fusion.9) | copy-start | bytes 1376260

commit v2 on v1

v2 whole, which is shorter than its diff:
```python
import functools

import jax
import jax.numpy as jnp
from jax import lax
from jax.experimental import pallas as pl
from jax.experimental.pallas import tpu as pltpu
from jax.sharding import PartitionSpec as P


NBASIS = 1152
NORB = 896
MINE = 28
WIDTH = 112
ROWS = 36
PAIRS = 64
COUNT = 32
LANES = ROWS * PAIRS
NEAR, FAR, LAST = 8, 16, 4
BOTH = ("pq", "rs")


def place(z_hi, x, y, z_lo, core):
    return (z_hi * 4 + x) * 32 + y * 8 + z_lo * 2 + core


ALONG_Z = [
    [place(h, x, y, z, c) for h in range(2) for z in range(4) for c in range(2)]
    for x in range(4)
    for y in range(4)
]
ACROSS = [
    [place(h, x, y, z, c) for x in range(4) for y in range(4)]
    for h in range(2)
    for z in range(4)
    for c in range(2)
]


def from_group(array, groups):
    copies = jnp.broadcast_to(array[None], (len(groups[0]), *array.shape))
    return lax.all_to_all(copies, BOTH, 0, 0, tiled=True, axis_index_groups=groups)


def iota(shape, dim):
    return lax.broadcasted_iota(jnp.int32, shape, dim)


def one_hot(match):
    return jnp.where(match, 1.0, 0.0).astype(jnp.bfloat16)


def pick(array, chosen):
    return jnp.dot(array, chosen, preferred_element_type=jnp.float32).astype(jnp.bfloat16)


def join_kernel(own_ref, a_ref, b_ref, c_ref, d_ref, out_ref):
    total = jnp.zeros(out_ref.shape, jnp.float32)
    for step, ref in enumerate((a_ref, b_ref, c_ref, d_ref)):
        for h in range(2):
            owner = h * 4 + (own_ref[0] ^ step)
            shape = (WIDTH, NORB)
            chosen = one_hot(iota(shape, 1) == owner * WIDTH + iota(shape, 0))
            total += jnp.dot(ref[h], chosen, preferred_element_type=jnp.float32)
    out_ref[...] = total.astype(out_ref.dtype)


def join(slabs, x):
    block = 576
    return pl.pallas_call(
        join_kernel,
        grid=(NBASIS // block,),
        in_specs=[pl.BlockSpec(memory_space=pltpu.SMEM)]
        + [pl.BlockSpec((2, block, WIDTH), lambda i: (0, i, 0))] * 4,
        out_specs=pl.BlockSpec((block, NORB), lambda i: (i, 0)),
        out_shape=jax.ShapeDtypeStruct((NBASIS, NORB), jnp.bfloat16),
        name="join",
    )(x.reshape(1), *slabs)


def early_kernel(own_ref, columns_ref, low_ref, high_ref, near_ref, *rest):
    *last_refs, part, turned = rest
    step = pl.program_id(0)
    edge = COUNT * NEAR

    @pl.when(step == 0)
    def _():
        for x in range(4):
            for h in range(2):
                for size, top, base in ((NEAR, 0, 0), (LAST, 4 * NEAR, edge)):
                    lines = 4 * size
                    strips = [
                        columns_ref[x * 4 + y, pl.ds(top, lines), pl.ds(h * 288, 288)]
                        for y in range(4)
                    ]
                    part[pl.ds(base + (h * 4 + x) * lines, lines), :] = jnp.concatenate(strips, 1)
        shape = (COUNT * LAST, COUNT * LAST)
        to, come = iota(shape, 0), iota(shape, 1)
        d = to // LAST
        d = (d & 6) << 2 | (d & 24) >> 2 | d & 1
        swap = one_hot((come // LAST == (d ^ own_ref[0])) & (come % LAST == to % LAST))
        last = jnp.dot(swap, part[edge:, :], preferred_element_type=jnp.float32)
        part[edge:, :] = last.astype(part.dtype)
        turned[...] = part[...].T

    lanes = pl.ds(pl.multiple_of(step * low_ref.shape[0], 128), low_ref.shape[0])
    lasts = []
    for half, ref in enumerate((low_ref, high_ref)):
        first = jnp.dot(ref[...], turned[...], preferred_element_type=jnp.float32)
        first = first.astype(jnp.bfloat16).T
        block = first.shape[1]
        at = pl.multiple_of(half * (LANES // 2) + step * block, 128)
        near_ref[:, :, pl.ds(at, block)] = first[:edge].reshape(COUNT, NEAR, block)
        lasts.append(first[edge:].astype(jnp.float32).reshape(COUNT, LAST, block))
    lasts = jnp.concatenate(lasts, 1).astype(jnp.bfloat16)
    for step, ref in enumerate(last_refs):
        ref[:, :, lanes] = lasts[8 * step : 8 * step + 8]


def early_first(columns, flat, own):
    block = 384
    steps = LANES // 2 // block
    return pl.pallas_call(
        early_kernel,
        grid=(steps,),
        in_specs=[
            pl.BlockSpec(memory_space=pltpu.SMEM),
            pl.BlockSpec(columns.shape, lambda i: (0, 0, 0)),
            pl.BlockSpec((block, NBASIS), lambda i: (i, 0)),
            pl.BlockSpec((block, NBASIS), lambda i: (i + steps, 0)),
        ],
        out_specs=[
            pl.BlockSpec((COUNT, NEAR, LANES), lambda i: (0, 0, 0)),
        ]
        + [pl.BlockSpec((8, 2 * LAST, LANES // 2), lambda i: (0, 0, 0))] * 4,
        out_shape=[
            jax.ShapeDtypeStruct((COUNT, NEAR, LANES), jnp.bfloat16),
        ]
        + [jax.ShapeDtypeStruct((8, 2 * LAST, LANES // 2), jnp.bfloat16)] * 4,
        scratch_shapes=[
            pltpu.VMEM((COUNT * (NEAR + LAST), NBASIS), jnp.bfloat16),
            pltpu.VMEM((NBASIS, COUNT * (NEAR + LAST)), jnp.bfloat16),
        ],
        name="early_first",
    )(own.reshape(1), columns, flat, flat)


def leave(part, flat):
    first = jnp.einsum("sc,ms->cm", part, flat, preferred_element_type=jnp.float32)
    return first.astype(jnp.bfloat16).reshape(COUNT, -1, LANES)


def slot_of(r, j):
    tile, odd = r // 2, r % 2
    return jnp.where(
        tile < 16, odd * 512 + tile * 32 + j, 1024 + odd * 64 + (tile - 16) * 32 + j
    )


def second_kernel(got_ref, panel_ref, *rest, halves):
    out_ref, wide, lhs = rest[-3:]
    count, lines, lanes = got_ref.shape
    mine = lines // halves
    tiles = lanes // 128
    for tile in range(tiles):
        piece = got_ref[:, :, pl.ds(tile * 128, 128)].astype(jnp.float32)
        wide[pl.ds(tile * count * lines, count * lines), :] = piece.reshape(count * lines, 128)
    for l in range(mine):
        rows = pl.ds(l * PAIRS, PAIRS)
        for start in range(0, 18, 4):
            parts = []
            for tile in range(start, min(start + 4, 18)):
                half, at = tile // tiles, tile % tiles
                top = at * count * lines + half * mine + l
                parts.append(wide[pl.ds(top, count, stride=lines), :])
            turned = jnp.concatenate(parts, 0).astype(jnp.bfloat16).T
            if len(parts) == 4:
                lhs[rows, pl.ds(start * 32, 128)] = turned[:PAIRS]
                lhs[rows, pl.ds(512 + start * 32, 128)] = turned[PAIRS:]
            else:
                lhs[rows, pl.ds(1024, 128)] = jnp.concatenate([turned[:PAIRS], turned[PAIRS:]], 1)
    product = jnp.dot(lhs[...], panel_ref[...], preferred_element_type=jnp.float32)
    out_ref[...] = product.astype(out_ref.dtype).reshape(out_ref.shape)


def second(got, ordered, into, lo, halves=1):
    count, lines, lanes = got.shape
    block = 8 // halves
    specs = [
        pl.BlockSpec((count, 8, lanes), lambda i: (0, i, 0)),
        pl.BlockSpec(ordered.shape, lambda i: (0, 0)),
    ]
    operands = [got, ordered]
    aliases = {}
    if into is not None:
        specs.append(pl.BlockSpec(memory_space=pl.ANY))
        operands.append(into)
        aliases = {2: 0}
    return pl.pallas_call(
        functools.partial(second_kernel, halves=halves),
        grid=(lines // 8,),
        in_specs=specs,
        out_specs=pl.BlockSpec((block, PAIRS, NORB), lambda i: (lo // block + i, 0, 0)),
        out_shape=jax.ShapeDtypeStruct((MINE, PAIRS, NORB), jnp.bfloat16),
        scratch_shapes=[
            pltpu.VMEM((count * 8 * lanes // 128, 128), jnp.float32),
            pltpu.VMEM((block * PAIRS, NBASIS), jnp.bfloat16),
        ],
        input_output_aliases=aliases,
        name="second",
    )(*operands)


def ordering(panel, place_of):
    shape = (NBASIS, NBASIS)
    slot = slot_of(iota(shape, 1) % ROWS, place_of(iota(shape, 1) // ROWS))
    return pick(one_hot(slot == iota(shape, 0)), panel)


def select(chosen, strip):
    columns = jnp.dot(chosen, strip.reshape(-1, WIDTH).T, preferred_element_type=jnp.float32)
    return columns.astype(jnp.bfloat16)


def on_device(integrals, coeff):
    x = lax.axis_index("pq") % 4
    own = lax.axis_index("rs")
    y = own // 8
    flat = integrals.transpose(1, 0, 2).reshape(LANES, NBASIS)

    strip = from_group(coeff, ALONG_Z).reshape(2, 8 * ROWS, WIDTH)

    shape = (4 * (NEAR + LAST), WIDTH)
    row, edge = iota(shape, 0), 4 * NEAR
    wanted = jnp.where(
        row < edge,
        row // NEAR * MINE + row % NEAR,
        (row - edge) // LAST * MINE + NEAR + FAR + (row - edge) % LAST,
    )
    columns = select(one_hot(iota(shape, 1) == wanted), strip)
    early = from_group(columns, ACROSS)
    near, *last = early_first(early, flat, own)

    stack = [strip]
    for step in (1, 2, 3):
        stack.append(lax.ppermute(strip, "rs", [(j, j ^ step * 8) for j in range(COUNT)]))
    low, high = y % 2 == 1, y // 2 == 1
    stack = [jnp.where(low, stack[i ^ 1], stack[i]) for i in range(4)]
    stack = jnp.stack([jnp.where(high, stack[i ^ 2], stack[i]) for i in range(4)], 1)
    slab = stack.reshape(2, NBASIS, WIDTH)
    slabs = [slab]
    for step in (1, 2, 3):
        slabs.append(lax.ppermute(slab, "pq", [(i, i & 4 | (i & 3) ^ step) for i in range(8)]))
    panel = join(slabs, x)

    got_near = lax.all_to_all(near, "rs", 0, 0, tiled=True)

    held = [last[0]]
    for step in (1, 2, 3):
        held.append(
            lax.ppermute(last[step], "rs", [(j, j ^ step * 2) for j in range(COUNT)])
        )
    held = jnp.stack(held, 1)
    got_last = [held[0]]
    for step in range(1, 8):
        got_last.append(
            lax.ppermute(
                held[step],
                "rs",
                [(j, j ^ (step // 2 * 8 + step % 2)) for j in range(COUNT)],
            )
        )
    got_last = jnp.concatenate(got_last, 0)

    shape = (NORB, COUNT * FAR)
    source = iota(shape, 1) // FAR * MINE + NEAR + iota(shape, 1) % FAR
    part = lax.optimization_barrier(pick(panel, one_hot(iota(shape, 0) == source)))
    far = leave(part, flat)
    got_far = lax.all_to_all(far, "rs", 0, 0, tiled=True)

    ordered = ordering(panel, lambda j: j)
    crossed = ordering(panel, lambda j: ((j ^ own) & 24) | ((j ^ own) & 1) << 2 | ((j ^ own) & 6) >> 1)
    out = second(got_near, ordered, None, 0)
    out = second(got_last, crossed, out, NEAR + FAR, halves=2)
    out = second(got_far, ordered, out, NEAR)
    return out.transpose(1, 0, 2)


def solution(mesh):
    placed = (P("pq", "rs", None), P("rs", "pq"))
    return jax.shard_map(
        on_device, mesh=mesh, in_specs=placed, out_specs=P("pq", "rs", None), check_vma=False
    )
```

time: 221 us -> 200 us (0.905)
  blocking collectives: 59.7 us -> 0 us
  starting transfers between devices: 28.6 us -> 59.5 us
  Pallas kernels: 6.96 us -> 29.6 us
  local copies, waits for them, and re-layouts: 22.6 us -> 9.7 us
  matrix products: 27.6 us -> 22.5 us
    all_to_all x2 -> x0, blocking collectives: 59.7 us -> none  [on_device(): got = lax.all_to_all(first, 'rs', 0, 0, tiled=True)]
    pallas_call x1 -> x5, Pallas kernels: 6.96 us -> 29.6 us  [the longest x3 15.3 us: second(): pl.pallas_call(functools.partial(second_kernel, halves=halves), grid=(lin...]
    ppermute x6 -> x16, starting transfers between devices: 7.26 us -> 25.9 us  [the longest x7 14.9 us: on_device(): lax.ppermute(held[step], 'rs', [(j, j ^ step // 2 * 8 + step % 2) for j i...]
    reshape x8 -> x2, local copies, waits for them, and re-layouts: 17.4 us -> 0.34 us  [the longest x1 0.29 us: on_device(): slab = stack.reshape(2, NBASIS, WIDTH)]
    all_to_all x1 -> x2, starting transfers between devices: 4.82 us -> 17.4 us  [the longest x1 13.5 us: on_device(): got_near = lax.all_to_all(near, 'rs', 0, 0, tiled=True)]
    dot_general x3 -> x1, matrix products: 12.1 us -> 0.26 us  [select(): jnp.dot(chosen, strip.reshape(-1, WIDTH).T, preferred_element_type=jnp.fl...]
    dot_general x3, matrix products: 4.1 us -> 14.5 us  [pick(): jnp.dot(array, chosen, preferred_element_type=jnp.float32)]
    ppermute x6 -> x16, waiting for transfers between devices: 17 us -> 25.7 us  [the longest x3 12.4 us: on_device(): lax.ppermute(slab, 'pq', [(i, i & 4 | i & 3 ^ step) for i in range(8)])]
  transfers between devices with their start and end apart: 9 -> 20, of which waited for: 5 -> 15; matrix products, arithmetic and copies ran while one was open for 11% -> 16% of each run, Pallas kernels for 0% -> 8%
where the time goes in v2:
time: 200 us; the launch traced here: 199 us
  waiting for transfers between devices  74.5 us (37%)
  starting transfers between devices  59.5 us (30%)
  Pallas kernels  29.6 us (15%)
  matrix products  22.5 us (11%)
  local copies, waits for them, and re-layouts  9.7 us (5%)
  other arithmetic  3.24 us (2%)
    all_to_all x1, waiting for transfers between devices, on_device(): got_near = lax.all_to_all(near, 'rs', 0, 0, tiled=True)  21.3 us
    all_to_all x1, waiting for transfers between devices, on_device(): got_far = lax.all_to_all(far, 'rs', 0, 0, tiled=True)  18.4 us
    all_to_all x2, starting transfers between devices, from_group(): lax.all_to_all(copies, BOTH, 0, 0, tiled=True, axis_index_groups=groups)  16.1 us
    pallas_call x3, Pallas kernels, second(): pl.pallas_call(functools.partial(second_kernel, halves=halves), grid=(lin...  15.3 us
    ppermute x7, starting transfers between devices, on_device(): lax.ppermute(held[step], 'rs', [(j, j ^ step // 2 * 8 + step % 2) for j i...  14.9 us
    dot_general x3, matrix products, pick(): jnp.dot(array, chosen, preferred_element_type=jnp.float32)  14.5 us
    all_to_all x1, starting transfers between devices, on_device(): got_near = lax.all_to_all(near, 'rs', 0, 0, tiled=True)  13.5 us
    ppermute x3, waiting for transfers between devices, on_device(): lax.ppermute(slab, 'pq', [(i, i & 4 | i & 3 ^ step) for i in range(8)])  12.4 us
  transfers between devices with their start and end apart: 20, of which 15 were waited for; matrix products, arithmetic and copies ran while one was open for 16% of the time, Pallas kernels for 8%

profile of v2, /device:TPU:1, one launch (start us, length us, event | category | flops | bytes accessed | tf_op | source)
XLA Modules:
  0.0 199.1 jit_solution(11310156115069237859)
XLA Ops:
  1.4 10.0 %all-to-all-start = ((bf16[16,36,112]{2,1,0:T(8,128)(2,1)}), bf16[16,36,112]{2,1,0:T(8,128)(2,1)S(1)}, u32[]{:S(2)}, u32[]{:S(2)}) async-start(bf16[16,36,112]{2,1,0:T(8,128)(2,1)} %broadcast_in_dim.38), calls=%async_computation | async-start | bytes 327680 | tf_op jit(solution)/shard_map/all_to_all | solution.py:42
  12.6 8.2 %all-to-all-done = bf16[16,36,112]{2,1,0:T(8,128)(2,1)S(1)} async-done(((bf16[16,36,112]{2,1,0:T(8,128)(2,1)}), bf16[16,36,112]{2,1,0:T(8,128)(2,1)S(1)}, u32[]{:S(2)}, u32[]{:S(2)}) %all-to-all-start) | async-done | bytes 129056 | tf_op jit(solution)/shard_map/all_to_all | solution.py:42
  20.9 2.8 %collective-permute-start = (bf16[2,288,112]{2,1,0:T(8,128)(2,1)S(1)}, bf16[2,288,112]{2,1,0:T(8,128)(2,1)S(1)}, u32[]{:S(2)}, u32[]{:S(2)}) collective-permute-start(bf16[2,288,112]{2,1,0:T(8,128)(2,1)S(1)} %reshape.21), channel_id=1, source_target_pairs={{0,24},{1,25},{2,26},{3,27},{4,28},{5,29},{6,30},{7,31},{8,16},{9,... | collective-permute-start | bytes 387080 | tf_op jit(solution)/shard_map/ppermute | solution.py:246
  24.5 5.9 %collective-permute-done = bf16[2,288,112]{2,1,0:T(8,128)(2,1)S(1)} collective-permute-done((bf16[2,288,112]{2,1,0:T(8,128)(2,1)S(1)}, bf16[2,288,112]{2,1,0:T(8,128)(2,1)S(1)}, u32[]{:S(2)}, u32[]{:S(2)}) %collective-permute-start) | collective-permute-done | bytes 129056 | tf_op jit(solution)/shard_map/ppermute | solution.py:246
  33.6 2.5 %collective-permute-start.4 = (bf16[2,1152,112]{1,2,0:T(8,128)(2,1)S(1)}, bf16[2,1152,112]{1,2,0:T(8,128)(2,1)S(1)}, u32[]{:S(2)}, u32[]{:S(2)}) collective-permute-start(bf16[2,1152,112]{1,2,0:T(8,128)(2,1)S(1)} %copy.10), channel_id=1, source_target_pairs={{0,64},{32,96},{64,0},{96,32},{128,192},{160,224},{192,128},{224,1... | collective-permute-start | bytes 1548296 | tf_op jit(solution)/shard_map/ppermute | solution.py:253
  37.5 6.2 %all-to-all-start.2 = ((bf16[16,48,576]{2,1,0:T(8,128)(2,1)}), bf16[16,48,576]{2,1,0:T(8,128)(2,1)S(1)}, u32[]{:S(2)}, u32[]{:S(2)}) async-start(bf16[16,48,576]{2,1,0:T(8,128)(2,1)} %broadcast_in_dim.45), calls=%async_computation.2 | async-start | bytes 1966080 | tf_op jit(solution)/shard_map/all_to_all | solution.py:42
  47.1 11.1 %collective-permute-done.4 = bf16[2,1152,112]{1,2,0:T(8,128)(2,1)S(1)} collective-permute-done((bf16[2,1152,112]{1,2,0:T(8,128)(2,1)S(1)}, bf16[2,1152,112]{1,2,0:T(8,128)(2,1)S(1)}, u32[]{:S(2)}, u32[]{:S(2)}) %collective-permute-start.4) | collective-permute-done | bytes 516128 | tf_op jit(solution)/shard_map/ppermute | solution.py:253
  61.0 6.8 %join.1 = bf16[1152,896]{1,0:T(8,128)(2,1)} custom-call(s32[1]{0:T(128)} %bitcast.own_ref, bf16[2,1152,112]{2,1,0:T(8,128)(2,1)} %bitcast.48, bf16[2,1152,112]{2,1,0:T(8,128)(2,1)} %copy.13.b_ref, bf16[2,1152,112]{2,1,0:T(8,128)(2,1)} %copy.14.c_ref, bf16[2,1152,112]{2,1,0:T(8,128)(2,1)} %copy.15.d_ref), custom_call_target="tpu_custom_call" | custom-call | tf_op jit(solution)/shard_map/join/pallas_call | solution.py:70
  67.9 4.0 %convolution_convert_fusion.3 = bf16[1152,512]{1,0:T(8,128)(2,1)} fusion(bf16[1152,896]{1,0:T(8,128)(2,1)} %join.1, s32[512]{0:T(512)S(1)} %get-tuple-element.27, s32[512]{0:T(512)S(1)} %get-tuple-element.28, s32[512]{0:T(512)S(1)} %get-tuple-element.26, s32[512]{0:T(512)S(1)} %get-tuple-element.29, pred[512]{0:T(512)(128)(4,1)S(1)} %get-tuple-element.31, ...), kind=kOutput, calls=%fused_computation.33 | convolution fusion | flops 1061224448 | bytes 3253248 | tf_op jit(solution)/shard_map/dot_general | solution.py:54
  73.7 7.4 %early_first.1 = (bf16[32,8,2304]{2,1,0:T(8,128)(2,1)}, bf16[8,8,1152]{2,1,0:T(8,128)(2,1)}, bf16[8,8,1152]{2,1,0:T(8,128)(2,1)}, bf16[8,8,1152]{2,1,0:T(8,128)(2,1)}, bf16[8,8,1152]{2,1,0:T(8,128)(2,1)}) custom-call(s32[1]{0:T(128)} %bitcast.9.own_ref, bf16[16,48,576]{2,1,0:T(8,128)(2,1)} %copy-done.3, bf16[2304,1152]{1,0:T(8,128)(2,1)} %bitcast.44, ...), custom_call_target="tpu_custom_call" | custom-call | tf_op jit(solution)/shard_map/early_first/pallas_call | solution.py:123
  81.1 13.5 %all-to-all-start.3 = ((bf16[32,8,2304]{2,1,0:T(8,128)(2,1)}), bf16[32,8,2304]{2,1,0:T(8,128)(2,1)S(1)}, u32[]{:S(2)}, u32[]{:S(2)}) async-start(bf16[32,8,2304]{2,1,0:T(8,128)(2,1)} %get-tuple-element.14), calls=%async_computation.3 | async-start | bytes 2359296 | tf_op jit(solution)/shard_map/all_to_all | solution.py:256
  94.7 7.7 %convolution_convert_fusion = bf16[512,2304]{1,0:T(8,128)(2,1)} fusion(bf16[1152,512]{1,0:T(8,128)(2,1)} %convolution_convert_fusion.3, bf16[2304,1152]{1,0:T(8,128)(2,1)} %bitcast.46), kind=kOutput, calls=%fused_computation.30 | convolution fusion | flops 2719088640 | bytes 8847360 | tf_op jit(solution)/shard_map/sc,ms->cm/dot_general | solution.py:149
  102.4 4.5 %convolution_convert_fusion.1.panel_ref = bf16[1152,896]{1,0:T(8,128)(2,1)} fusion(bf16[1152,896]{1,0:T(8,128)(2,1)S(1)} %copy-done.4, s32[]{:T(128)} %axis_index.25, s32[1152]{0:T(1024)S(1)} %get-tuple-element.32, s32[1152]{0:T(1024)S(1)} %copy-done.8, pred[1152]{0:T(1024)(128)(4,1)S(1)} %copy-done.9, s32[1152]{0:T(1024)S(1)} %copy-done.7, ...), kind=kOutput, calls=%fused_computation.31 | convolution fusion | flops 2437595136 | bytes 4149508 | tf_op jit(solution)/shard_map/dot_general | solution.py:54
  110.5 21.3 %all-to-all-done.3.got_ref = bf16[32,8,2304]{2,1,0:T(8,128)(2,1)S(1)} async-done(((bf16[32,8,2304]{2,1,0:T(8,128)(2,1)}), bf16[32,8,2304]{2,1,0:T(8,128)(2,1)S(1)}, u32[]{:S(2)}, u32[]{:S(2)}) %all-to-all-start.3) | async-done | bytes 1179680 | tf_op jit(solution)/shard_map/all_to_all | solution.py:256
  131.8 3.8 %all-to-all-start.1 = ((bf16[32,16,2304]{2,1,0:T(8,128)(2,1)}), bf16[32,16,2304]{2,1,0:T(8,128)(2,1)S(1)}, u32[]{:S(2)}, u32[]{:S(2)}) async-start(bf16[32,16,2304]{2,1,0:T(8,128)(2,1)} %bitcast.49), calls=%async_computation.1 | async-start | bytes 4718592 | tf_op jit(solution)/shard_map/all_to_all | solution.py:279
  135.6 6.0 %convolution_convert_fusion.2.panel_ref = bf16[1152,896]{1,0:T(8,128)(2,1)} fusion(bf16[1152,896]{1,0:T(8,128)(2,1)} %join.1, s32[1152]{0:T(1024)S(1)} %get-tuple-element.32, s32[1152]{0:T(1024)} %get-tuple-element.35, pred[1152]{0:T(1024)(128)(4,1)} %fusion.50, s32[1152]{0:T(1024)} %get-tuple-element.34, s32[1152]{0:T(1024)S(1)} %get-tuple-element.33, ...), kind=kOutput, calls=%fused_computation.32 | convolution fusion | flops 2426978304 | bytes 4149504 | tf_op jit(solution)/shard_map/dot_general | solution.py:54
  145.1 3.0 %collective-permute-start.12 = (bf16[4,8,1152]{2,1,0:T(8,128)(2,1)S(1)}, bf16[4,8,1152]{2,1,0:T(8,128)(2,1)S(1)}, u32[]{:S(2)}, u32[]{:S(2)}) collective-permute-start(bf16[4,8,1152]{2,1,0:T(8,128)(2,1)S(1)} %get-tuple-element.18), channel_id=1, source_target_pairs={{0,16},{1,17},{2,18},{3,19},{4,20},{5,21},{6,22},{7,23},{8,24},{9,... | collective-permute-start | bytes 221192 | tf_op jit(solution)/shard_map/ppermute | solution.py:267
  148.4 2.7 %collective-permute-start.14 = (bf16[4,8,1152]{2,1,0:T(8,128)(2,1)S(1)}, bf16[4,8,1152]{2,1,0:T(8,128)(2,1)S(1)}, u32[]{:S(2)}, u32[]{:S(2)}) collective-permute-start(bf16[4,8,1152]{2,1,0:T(8,128)(2,1)S(1)} %get-tuple-element.16), channel_id=1, source_target_pairs={{0,24},{1,25},{2,26},{3,27},{4,28},{5,29},{6,30},{7,31},{8,16},{9,... | collective-permute-start | bytes 221192 | tf_op jit(solution)/shard_map/ppermute | solution.py:267
  151.7 6.8 %collective-permute-start.15 = (bf16[4,8,1152]{2,1,0:T(8,128)(2,1)S(1)}, bf16[4,8,1152]{2,1,0:T(8,128)(2,1)S(1)}, u32[]{:S(2)}, u32[]{:S(2)}) collective-permute-start(bf16[4,8,1152]{2,1,0:T(8,128)(2,1)S(1)} %get-tuple-element.15), channel_id=1, source_target_pairs={{0,25},{1,24},{2,27},{3,26},{4,29},{5,28},{6,31},{7,30},{8,17},{9,... | collective-permute-start | bytes 221192 | tf_op jit(solution)/shard_map/ppermute | solution.py:267
  160.7 2.5 %collective-permute-done.13 = bf16[4,8,1152]{2,1,0:T(8,128)(2,1)S(1)} collective-permute-done((bf16[4,8,1152]{2,1,0:T(8,128)(2,1)S(1)}, bf16[4,8,1152]{2,1,0:T(8,128)(2,1)S(1)}, u32[]{:S(2)}, u32[]{:S(2)}) %collective-permute-start.13) | collective-permute-done | bytes 73760 | tf_op jit(solution)/shard_map/ppermute | solution.py:267
  164.0 5.0 %second.3.rest_0_ = bf16[28,64,896]{2,1,0:T(8,128)(2,1)} custom-call(bf16[32,8,2304]{2,1,0:T(8,128)(2,1)} %copy-done.2, bf16[1152,896]{1,0:T(8,128)(2,1)} %convolution_convert_fusion.2.panel_ref), custom_call_target="tpu_custom_call" | custom-call | tf_op jit(solution)/shard_map/second/pallas_call | solution.py:199
  169.0 3.6 %second.4.rest_0_ = bf16[28,64,896]{2,1,0:T(8,128)(2,1)} custom-call(bf16[32,8,1152]{2,1,0:T(8,128)(2,1)} %copy-done.5, bf16[1152,896]{1,0:T(8,128)(2,1)} %convolution_convert_fusion.1.panel_ref, bf16[28,64,896]{2,1,0:T(8,128)(2,1)} %second.3.rest_0_), custom_call_target="tpu_custom_call", output_to_operand_aliasing={{}: (2, {})} | custom-call | tf_op jit(solution)/shard_map/second/pallas_call | solution.py:199
  172.6 18.4 %all-to-all-done.1.got_ref = bf16[32,16,2304]{2,1,0:T(8,128)(2,1)S(1)} async-done(((bf16[32,16,2304]{2,1,0:T(8,128)(2,1)}), bf16[32,16,2304]{2,1,0:T(8,128)(2,1)S(1)}, u32[]{:S(2)}, u32[]{:S(2)}) %all-to-all-start.1) | async-done | bytes 2359328 | tf_op jit(solution)/shard_map/all_to_all | solution.py:279
  192.4 6.7 %second.5 = bf16[28,64,896]{2,1,0:T(8,128)(2,1)} custom-call(bf16[32,16,2304]{2,1,0:T(8,128)(2,1)} %copy-done, bf16[1152,896]{1,0:T(8,128)(2,1)} %convolution_convert_fusion.2.panel_ref, bf16[28,64,896]{2,1,0:T(8,128)(2,1)} %second.4.rest_0_), custom_call_target="tpu_custom_call", output_to_operand_aliasing={{}: (2, {})} | custom-call | tf_op jit(solution)/shard_map/second/pallas_call | solution.py:199
  (83 shorter events, 28.5 us)
Async XLA Ops:
  1.4 19.5 %all-to-all-start = ((bf16[16,36,112]{2,1,0:T(8,128)(2,1)}), bf16[16,36,112]{2,1,0:T(8,128)(2,1)S(1)}, u32[]{:S(2)}, u32[]{:S(2)}) async-start(bf16[16,36,112]{2,1,0:T(8,128)(2,1)} %broadcast_in_dim.38), calls=%async_computation | async-start | bytes 327680 | tf_op jit(solution)/shard_map/all_to_all | solution.py:42
  20.9 9.4 %collective-permute-start = (bf16[2,288,112]{2,1,0:T(8,128)(2,1)S(1)}, bf16[2,288,112]{2,1,0:T(8,128)(2,1)S(1)}, u32[]{:S(2)}, u32[]{:S(2)}) collective-permute-start(bf16[2,288,112]{2,1,0:T(8,128)(2,1)S(1)} %reshape.21), channel_id=1, source_target_pairs={{0,24},{1,25},{2,26},{3,27},{4,28},{5,29},{6,30},{7,31},{8,16},{9,... | collective-permute-start | bytes 387080 | tf_op jit(solution)/shard_map/ppermute | solution.py:246
  23.8 6.9 %collective-permute-start.1 = (bf16[2,288,112]{2,1,0:T(8,128)(2,1)S(1)}, bf16[2,288,112]{2,1,0:T(8,128)(2,1)S(1)}, u32[]{:S(2)}, u32[]{:S(2)}) collective-permute-start(bf16[2,288,112]{2,1,0:T(8,128)(2,1)S(1)} %reshape.21), channel_id=1, source_target_pairs={{0,16},{1,17},{2,18},{3,19},{4,20},{5,21},{6,22},{7,23},{8,24},{9,... | collective-permute-start | bytes 387080 | tf_op jit(solution)/shard_map/ppermute | solution.py:246
  24.1 7.6 %collective-permute-start.2 = (bf16[2,288,112]{2,1,0:T(8,128)(2,1)S(1)}, bf16[2,288,112]{2,1,0:T(8,128)(2,1)S(1)}, u32[]{:S(2)}, u32[]{:S(2)}) collective-permute-start(bf16[2,288,112]{2,1,0:T(8,128)(2,1)S(1)} %reshape.21), channel_id=1, source_target_pairs={{0,8},{1,9},{2,10},{3,11},{4,12},{5,13},{6,14},{7,15},{8,0},{9,1},... | collective-permute-start | bytes 387080 | tf_op jit(solution)/shard_map/ppermute | solution.py:246
  32.0 29.1 %copy-start.1 = (bf16[2,4,288,112]{3,2,1,0:T(8,128)(2,1)}, bf16[2,4,288,112]{3,2,1,0:T(8,128)(2,1)S(1)}, u32[]{:S(2)}) copy-start(bf16[2,4,288,112]{3,2,1,0:T(8,128)(2,1)S(1)} %copy.9) | copy-start | bytes 1548292
  32.3 12.8 %collective-permute-start.3 = (bf16[2,1152,112]{1,2,0:T(8,128)(2,1)S(1)}, bf16[2,1152,112]{1,2,0:T(8,128)(2,1)}, u32[]{:S(2)}, u32[]{:S(2)}) collective-permute-start(bf16[2,1152,112]{1,2,0:T(8,128)(2,1)S(1)} %copy.10), channel_id=1, source_target_pairs={{0,32},{32,0},{64,96},{96,64},{128,160},{160,128},{192,224},{224,1... | collective-permute-start | bytes 1548296 | tf_op jit(solution)/shard_map/ppermute | solution.py:253
  33.6 24.6 %collective-permute-start.4 = (bf16[2,1152,112]{1,2,0:T(8,128)(2,1)S(1)}, bf16[2,1152,112]{1,2,0:T(8,128)(2,1)S(1)}, u32[]{:S(2)}, u32[]{:S(2)}) collective-permute-start(bf16[2,1152,112]{1,2,0:T(8,128)(2,1)S(1)} %copy.10), channel_id=1, source_target_pairs={{0,64},{32,96},{64,0},{96,32},{128,192},{160,224},{192,128},{224,1... | collective-permute-start | bytes 1548296 | tf_op jit(solution)/shard_map/ppermute | solution.py:253
  36.0 23.9 %collective-permute-start.5 = (bf16[2,1152,112]{1,2,0:T(8,128)(2,1)S(1)}, bf16[2,1152,112]{1,2,0:T(8,128)(2,1)S(1)}, u32[]{:S(2)}, u32[]{:S(2)}) collective-permute-start(bf16[2,1152,112]{1,2,0:T(8,128)(2,1)S(1)} %copy.10), channel_id=1, source_target_pairs={{0,96},{32,64},{64,32},{96,0},{128,224},{160,192},{192,160},{224,1... | collective-permute-start | bytes 1548296 | tf_op jit(solution)/shard_map/ppermute | solution.py:253
  37.5 35.2 %all-to-all-start.2 = ((bf16[16,48,576]{2,1,0:T(8,128)(2,1)}), bf16[16,48,576]{2,1,0:T(8,128)(2,1)S(1)}, u32[]{:S(2)}, u32[]{:S(2)}) async-start(bf16[16,48,576]{2,1,0:T(8,128)(2,1)} %broadcast_in_dim.45), calls=%async_computation.2 | async-start | bytes 1966080 | tf_op jit(solution)/shard_map/all_to_all | solution.py:42
  81.1 50.6 %all-to-all-start.3 = ((bf16[32,8,2304]{2,1,0:T(8,128)(2,1)}), bf16[32,8,2304]{2,1,0:T(8,128)(2,1)S(1)}, u32[]{:S(2)}, u32[]{:S(2)}) async-start(bf16[32,8,2304]{2,1,0:T(8,128)(2,1)} %get-tuple-element.14), calls=%async_computation.3 | async-start | bytes 2359296 | tf_op jit(solution)/shard_map/all_to_all | solution.py:256
  94.7 7.7 %copy-start.4 = (bf16[1152,896]{1,0:T(8,128)(2,1)S(1)}, bf16[1152,896]{1,0:T(8,128)(2,1)}, u32[]{:S(2)}) copy-start(bf16[1152,896]{1,0:T(8,128)(2,1)} %join.1) | copy-start | bytes 6193156
  94.7 7.7 %copy-start.7 = (s32[1152]{0:T(1024)S(1)}, s32[1152]{0:T(1024)}, u32[]{:S(2)}) copy-start(s32[1152]{0:T(1024)} %get-tuple-element.34) | copy-start | bytes 13828
  106.9 34.7 %collective-permute-start.6 = (bf16[8,8,1152]{2,1,0:T(8,128)(2,1)}, bf16[8,8,1152]{2,1,0:T(8,128)(2,1)}, u32[]{:S(2)}, u32[]{:S(2)}) collective-permute-start(bf16[8,8,1152]{2,1,0:T(8,128)(2,1)} %get-tuple-element.11), channel_id=1, source_target_pairs={{0,2},{1,3},{2,0},{3,1},{4,6},{5,7},{6,4},{7,5},{8,10},{9,11},{10,... | collective-permute-start | bytes 442376 | tf_op jit(solution)/shard_map/ppermute | solution.py:261
  108.3 33.4 %collective-permute-start.7 = (bf16[8,8,1152]{2,1,0:T(8,128)(2,1)}, bf16[8,8,1152]{2,1,0:T(8,128)(2,1)}, u32[]{:S(2)}, u32[]{:S(2)}) collective-permute-start(bf16[8,8,1152]{2,1,0:T(8,128)(2,1)} %get-tuple-element.12), channel_id=1, source_target_pairs={{0,4},{1,5},{2,6},{3,7},{4,0},{5,1},{6,2},{7,3},{8,12},{9,13},{10,... | collective-permute-start | bytes 442376 | tf_op jit(solution)/shard_map/ppermute | solution.py:261
  110.4 31.3 %collective-permute-start.8 = (bf16[8,8,1152]{2,1,0:T(8,128)(2,1)}, bf16[8,8,1152]{2,1,0:T(8,128)(2,1)}, u32[]{:S(2)}, u32[]{:S(2)}) collective-permute-start(bf16[8,8,1152]{2,1,0:T(8,128)(2,1)} %get-tuple-element.13), channel_id=1, source_target_pairs={{0,6},{1,7},{2,4},{3,5},{4,2},{5,3},{6,0},{7,1},{8,14},{9,15},{10,... | collective-permute-start | bytes 442376 | tf_op jit(solution)/shard_map/ppermute | solution.py:261
  131.8 9.9 %copy-start.2 = (bf16[32,8,2304]{2,1,0:T(8,128)(2,1)}, bf16[32,8,2304]{2,1,0:T(8,128)(2,1)S(1)}, u32[]{:S(2)}) copy-start(bf16[32,8,2304]{2,1,0:T(8,128)(2,1)S(1)} %all-to-all-done.3.got_ref) | copy-start | bytes 3538948
  131.8 59.2 %all-to-all-start.1 = ((bf16[32,16,2304]{2,1,0:T(8,128)(2,1)}), bf16[32,16,2304]{2,1,0:T(8,128)(2,1)S(1)}, u32[]{:S(2)}, u32[]{:S(2)}) async-start(bf16[32,16,2304]{2,1,0:T(8,128)(2,1)} %bitcast.49), calls=%async_computation.1 | async-start | bytes 4718592 | tf_op jit(solution)/shard_map/all_to_all | solution.py:279
  142.9 5.5 %collective-permute-start.9 = (bf16[4,8,1152]{2,1,0:T(8,128)(2,1)S(1)}, bf16[4,8,1152]{2,1,0:T(8,128)(2,1)S(1)}, u32[]{:S(2)}, u32[]{:S(2)}) collective-permute-start(bf16[4,8,1152]{2,1,0:T(8,128)(2,1)S(1)} %get-tuple-element.21), channel_id=1, source_target_pairs={{0,1},{1,0},{2,3},{3,2},{4,5},{5,4},{6,7},{7,6},{8,9},{9,8},{10,11... | collective-permute-start | bytes 221192 | tf_op jit(solution)/shard_map/ppermute | solution.py:267
  143.3 8.4 %collective-permute-start.10 = (bf16[4,8,1152]{2,1,0:T(8,128)(2,1)S(1)}, bf16[4,8,1152]{2,1,0:T(8,128)(2,1)S(1)}, u32[]{:S(2)}, u32[]{:S(2)}) collective-permute-start(bf16[4,8,1152]{2,1,0:T(8,128)(2,1)S(1)} %get-tuple-element.20), channel_id=1, source_target_pairs={{0,8},{1,9},{2,10},{3,11},{4,12},{5,13},{6,14},{7,15},{8,0},{9,1},... | collective-permute-start | bytes 221192 | tf_op jit(solution)/shard_map/ppermute | solution.py:267
  144.7 14.0 %collective-permute-start.11 = (bf16[4,8,1152]{2,1,0:T(8,128)(2,1)S(1)}, bf16[4,8,1152]{2,1,0:T(8,128)(2,1)S(1)}, u32[]{:S(2)}, u32[]{:S(2)}) collective-permute-start(bf16[4,8,1152]{2,1,0:T(8,128)(2,1)S(1)} %get-tuple-element.19), channel_id=1, source_target_pairs={{0,9},{1,8},{2,11},{3,10},{4,13},{5,12},{6,15},{7,14},{8,1},{9,0},... | collective-permute-start | bytes 221192 | tf_op jit(solution)/shard_map/ppermute | solution.py:267
  145.1 15.5 %collective-permute-start.12 = (bf16[4,8,1152]{2,1,0:T(8,128)(2,1)S(1)}, bf16[4,8,1152]{2,1,0:T(8,128)(2,1)S(1)}, u32[]{:S(2)}, u32[]{:S(2)}) collective-permute-start(bf16[4,8,1152]{2,1,0:T(8,128)(2,1)S(1)} %get-tuple-element.18), channel_id=1, source_target_pairs={{0,16},{1,17},{2,18},{3,19},{4,20},{5,21},{6,22},{7,23},{8,24},{9,... | collective-permute-start | bytes 221192 | tf_op jit(solution)/shard_map/ppermute | solution.py:267
  148.1 15.1 %collective-permute-start.13 = (bf16[4,8,1152]{2,1,0:T(8,128)(2,1)S(1)}, bf16[4,8,1152]{2,1,0:T(8,128)(2,1)S(1)}, u32[]{:S(2)}, u32[]{:S(2)}) collective-permute-start(bf16[4,8,1152]{2,1,0:T(8,128)(2,1)S(1)} %get-tuple-element.17), channel_id=1, source_target_pairs={{0,17},{1,16},{2,19},{3,18},{4,21},{5,20},{6,23},{7,22},{8,25},{9,... | collective-permute-start | bytes 221192 | tf_op jit(solution)/shard_map/ppermute | solution.py:267
  148.4 14.8 %collective-permute-start.14 = (bf16[4,8,1152]{2,1,0:T(8,128)(2,1)S(1)}, bf16[4,8,1152]{2,1,0:T(8,128)(2,1)S(1)}, u32[]{:S(2)}, u32[]{:S(2)}) collective-permute-start(bf16[4,8,1152]{2,1,0:T(8,128)(2,1)S(1)} %get-tuple-element.16), channel_id=1, source_target_pairs={{0,24},{1,25},{2,26},{3,27},{4,28},{5,29},{6,30},{7,31},{8,16},{9,... | collective-permute-start | bytes 221192 | tf_op jit(solution)/shard_map/ppermute | solution.py:267
  151.7 12.3 %collective-permute-start.15 = (bf16[4,8,1152]{2,1,0:T(8,128)(2,1)S(1)}, bf16[4,8,1152]{2,1,0:T(8,128)(2,1)S(1)}, u32[]{:S(2)}, u32[]{:S(2)}) collective-permute-start(bf16[4,8,1152]{2,1,0:T(8,128)(2,1)S(1)} %get-tuple-element.15), channel_id=1, source_target_pairs={{0,25},{1,24},{2,27},{3,26},{4,29},{5,28},{6,31},{7,30},{8,17},{9,... | collective-permute-start | bytes 221192 | tf_op jit(solution)/shard_map/ppermute | solution.py:267
  (7 other events, 36.6 us)

commit v3 on v0

v3 whole, which is shorter than its diff:
```python
import functools

import jax
import jax.numpy as jnp
from jax import lax
from jax.experimental import pallas as pl
from jax.experimental.pallas import tpu as pltpu
from jax.sharding import PartitionSpec as P


NBASIS = 1152
NORB = 896
MINE = 28
WIDTH = 112
ROWS = 36
PAIRS = 64
COUNT = 32
LANES = ROWS * PAIRS
SOON, FAR = 2, 5
HALF = LANES // 2
BOTH = ("pq", "rs")


def place(z_hi, x, y, z_lo, core):
    return (z_hi * 4 + x) * 32 + y * 8 + z_lo * 2 + core


ALONG_Z = [
    [place(h, x, y, z, c) for h in range(2) for z in range(4) for c in range(2)]
    for x in range(4)
    for y in range(4)
]


def from_group(array, groups):
    copies = jnp.broadcast_to(array[None], (len(groups[0]), *array.shape))
    return lax.all_to_all(copies, BOTH, 0, 0, tiled=True, axis_index_groups=groups)


def iota(shape, dim):
    return lax.broadcasted_iota(jnp.int32, shape, dim)


def one_hot(match):
    return jnp.where(match, 1.0, 0.0).astype(jnp.bfloat16)


def pick(array, chosen):
    return jnp.dot(array, chosen, preferred_element_type=jnp.float32).astype(jnp.bfloat16)


def spot(d, own):
    return ((d & 6) << 2 | (d & 24) >> 2 | d & 1) ^ own


def first_kernel(
    own_ref, x_ref, a_ref, b_ref, c_ref, d_ref, low_ref, high_ref, *rest, groups, permuted
):
    *near_refs, part, turned = rest
    near_refs, far_refs = (near_refs[:4], ()) if permuted else ((), near_refs)
    block = low_ref.shape[0]

    @pl.when(pl.program_id(0) == 0)
    def _():
        y = own_ref[0] >> 3
        for step, ref in enumerate((a_ref, b_ref, c_ref, d_ref)):
            for h in range(2):
                strips = [ref[y ^ k, :, pl.ds(h * 288, 288)] for k in range(4)]
                rows = jnp.concatenate(strips, 1)
                for group in range(groups):
                    top = group * 128 + (h * 4 + (x_ref[0] ^ step)) * 16
                    part[pl.ds(pl.multiple_of(top, 16), 16), :] = rows[group * 16 : group * 16 + 16]
        shape = (COUNT * 4, COUNT * 4)
        to, come = iota(shape, 0), iota(shape, 1)
        swap = one_hot((come // 4 == spot(to // 4, own_ref[0])) & (come % 4 == to % 4))
        for group in range(groups if permuted else 0):
            at = pl.ds(group * 128, 128)
            moved = jnp.dot(swap, part[at, :], preferred_element_type=jnp.float32)
            part[at, :] = moved.astype(part.dtype)
        turned[...] = part[...].T

    firsts = []
    for ref in (low_ref, high_ref):
        first = jnp.dot(ref[...], turned[...], preferred_element_type=jnp.float32).T
        firsts.append(first.reshape(groups, COUNT, 4, block))
    firsts = jnp.concatenate(firsts, 2).astype(jnp.bfloat16)
    for group in range(groups):
        at = pl.ds(pl.multiple_of(group * HALF + pl.program_id(0) * block, 128), block)
        for step, ref in enumerate(near_refs):
            ref[:, :, at] = firsts[group, 8 * step : 8 * step + 8]
        for ref in far_refs:
            ref[:, :, at] = firsts[group]


def first_product(slabs, flat, own, x, permuted):
    block = 384
    steps = HALF // block
    groups = slabs[0].shape[1] // 16
    shapes = [(8, 8, groups * HALF)] * 4 if permuted else [(COUNT, 8, groups * HALF)]
    whole = lambda shape: pl.BlockSpec(shape, lambda i: (0,) * len(shape))
    shapes.append((groups * 128, NBASIS))
    return pl.pallas_call(
        functools.partial(first_kernel, groups=groups, permuted=permuted),
        grid=(steps,),
        in_specs=[pl.BlockSpec(memory_space=pltpu.SMEM)] * 2
        + [whole(slabs[0].shape)] * 4
        + [
            pl.BlockSpec((block, NBASIS), lambda i: (i, 0)),
            pl.BlockSpec((block, NBASIS), lambda i: (i + steps, 0)),
        ],
        out_specs=[whole(shape) for shape in shapes],
        out_shape=[jax.ShapeDtypeStruct(shape, jnp.bfloat16) for shape in shapes],
        scratch_shapes=[pltpu.VMEM((NBASIS, groups * 128), jnp.bfloat16)],
    )(own.reshape(1), x.reshape(1), *slabs, flat, flat)


def slot_of(r, j):
    tile, odd = r // 2, r % 2
    return jnp.where(
        tile < 16, odd * 512 + tile * 32 + j, 1024 + odd * 64 + (tile - 16) * 32 + j
    )


def second_kernel(got_ref, panel_ref, *rest):
    out_ref, wide, lhs = rest[-3:]
    size = COUNT * 8
    for tile in range(HALF // 128):
        piece = got_ref[:, :, pl.ds(tile * 128, 128)].astype(jnp.float32)
        wide[pl.ds(tile * size, size), :] = piece.reshape(size, 128)
    for l in range(4):
        rows = pl.ds(l * PAIRS, PAIRS)
        for start in range(0, 18, 4):
            parts = []
            for tile in range(start, min(start + 4, 18)):
                top = tile % 9 * size + tile // 9 * 4 + l
                parts.append(wide[pl.ds(top, COUNT, stride=8), :])
            turned = jnp.concatenate(parts, 0).astype(jnp.bfloat16).T
            if len(parts) == 4:
                lhs[rows, pl.ds(start * 32, 128)] = turned[:PAIRS]
                lhs[rows, pl.ds(512 + start * 32, 128)] = turned[PAIRS:]
            else:
                lhs[rows, pl.ds(1024, 128)] = jnp.concatenate([turned[:PAIRS], turned[PAIRS:]], 1)
    product = jnp.dot(lhs[...], panel_ref[...], preferred_element_type=jnp.float32)
    out_ref[...] = product.astype(out_ref.dtype).reshape(out_ref.shape)


def second(got, ordered, into, lo):
    specs = [
        pl.BlockSpec((COUNT, 8, HALF), lambda i: (0, 0, i)),
        pl.BlockSpec(ordered.shape, lambda i: (0, 0)),
    ]
    operands = [got, ordered]
    aliases = {}
    if into is not None:
        specs.append(pl.BlockSpec(memory_space=pl.ANY))
        operands.append(into)
        aliases = {2: 0}
    return pl.pallas_call(
        second_kernel,
        grid=(got.shape[2] // HALF,),
        in_specs=specs,
        out_specs=pl.BlockSpec((4, PAIRS, NORB), lambda i: (lo + i, 0, 0)),
        out_shape=jax.ShapeDtypeStruct((MINE, PAIRS, NORB), jnp.bfloat16),
        scratch_shapes=[
            pltpu.VMEM((COUNT * 8 * HALF // 128, 128), jnp.float32),
            pltpu.VMEM((4 * PAIRS, NBASIS), jnp.bfloat16),
        ],
        input_output_aliases=aliases,
        name="second",
    )(*operands)


def ordering(panel, place_of):
    shape = (NBASIS, NBASIS)
    slot = slot_of(iota(shape, 1) % ROWS, place_of(iota(shape, 1) // ROWS))
    return pick(one_hot(slot == iota(shape, 0)), panel)


def columns_of(first, groups, strip):
    shape = (16 * groups, WIDTH)
    row = iota(shape, 0)
    column = row % 16 // 4 * MINE + (first + row // 16) * 4 + row % 4
    chosen = one_hot(iota(shape, 1) == column)
    rows = jnp.dot(chosen, strip.reshape(-1, WIDTH).T, preferred_element_type=jnp.float32)
    return rows.astype(jnp.bfloat16)


def spread(first):
    held = [first[0]]
    for step in (1, 2, 3):
        held.append(lax.ppermute(first[step], "rs", [(j, j ^ step * 2) for j in range(COUNT)]))
    held = jnp.stack(held, 1)
    got = [held[0]]
    for step in range(1, 8):
        pairs = [(j, j ^ (step // 2 * 8 + step % 2)) for j in range(COUNT)]
        got.append(lax.ppermute(held[step], "rs", pairs))
    return jnp.concatenate(got, 0)


def on_device(integrals, coeff):
    x = lax.axis_index("pq") % 4
    own = lax.axis_index("rs")
    flat = integrals.transpose(1, 0, 2).reshape(LANES, NBASIS)

    strip = from_group(coeff, ALONG_Z).reshape(2, 8 * ROWS, WIDTH)
    columns = columns_of(0, SOON + FAR, strip)
    slab = [columns]
    for step in (1, 2, 3):
        slab.append(lax.ppermute(columns, "rs", [(j, j ^ step * 8) for j in range(COUNT)]))

    def over_x(lo, hi):
        own_slab = jnp.stack([part[lo * 16 : hi * 16] for part in slab])
        slabs = [own_slab]
        for step in (1, 2, 3):
            pairs = [(i, i & 4 | (i & 3) ^ step) for i in range(8)]
            slabs.append(lax.ppermute(own_slab, "pq", pairs))
        return slabs

    early = over_x(0, SOON)
    late = over_x(SOON, SOON + FAR)
    *soon, soon_part = first_product(early, flat, own, x, True)
    far, far_part = first_product(late, flat, own, x, False)

    got_soon = spread(soon)
    got_far = lax.all_to_all(far, "rs", 0, 0, tiled=True)

    far_part, mine = lax.optimization_barrier((far_part, own))
    parts = jnp.concatenate([soon_part, far_part], 0)
    g = iota((NORB, NORB), 0)
    d = g % 128 // 4
    j = jnp.where(g < SOON * 128, spot(d, mine), d)
    put = one_hot(iota((NORB, NORB), 1) == j * MINE + g // 128 * 4 + g % 4)
    panel = jnp.einsum("gs,gk->sk", parts, put, preferred_element_type=jnp.float32)
    panel = panel.astype(jnp.bfloat16)
    ordered = ordering(panel, lambda j: j)
    crossed = ordering(
        panel, lambda j: ((j ^ mine) & 24) | ((j ^ mine) & 1) << 2 | ((j ^ mine) & 6) >> 1
    )
    out = second(got_soon, crossed, None, 0)
    out = second(got_far, ordered, out, SOON)
    return out.transpose(1, 0, 2)


def solution(mesh):
    placed = (P("pq", "rs", None), P("rs", "pq"))
    return jax.shard_map(
        on_device, mesh=mesh, in_specs=placed, out_specs=P("pq", "rs", None), check_vma=False
    )
```

time: 257 us -> 175 us (0.68)
  blocking collectives: 120 us -> 0 us
  local copies, waits for them, and re-layouts: 70.4 us -> 10.7 us
  waiting for transfers between devices: 37.1 us -> 75.5 us
  starting transfers between devices: 8.09 us -> 38.6 us
  Pallas kernels: 0 us -> 29.3 us
  other arithmetic: 0 us -> 6.11 us
  matrix products: 19.8 us -> 13.8 us
    all_to_all x2 -> x0, blocking collectives: 120 us -> none  [the longest x1 99.3 us: on_device(): lax.all_to_all(first, 'rs', split_axis=2, concat_axis=1, tiled=True)]
    ppermute x0 -> x19, waiting for transfers between devices: none -> 52.2 us  [the longest x6 22.9 us: over_x(): slabs.append(lax.ppermute(own_slab, 'pq', pairs))]
    reshape x4 -> x0, local copies, waits for them, and re-layouts: 31.6 us -> none  [the longest x2 20.8 us: on_device(): first = first.reshape(pair_rows, block_rows, NORB)]
    pallas_call x0 -> x4, Pallas kernels: none -> 29.3 us  [the longest x2 16.5 us: first_product(): pl.pallas_call(functools.partial(first_kernel, groups=groups, permuted=pe...]
    unnamed x3 -> x35, local copies, waits for them, and re-layouts: 36.4 us -> 8.46 us
    ppermute x0 -> x19, starting transfers between devices: none -> 20.4 us  [the longest x7 6.9 us: spread(): got.append(lax.ppermute(held[step], 'rs', pairs))]
    all_to_all x1 -> x2, waiting for transfers between devices: 37.1 us -> 23.4 us  [the longest x1 16.9 us: on_device(): got_far = lax.all_to_all(far, 'rs', 0, 0, tiled=True)]
    all_to_all x1 -> x2, starting transfers between devices: 8.09 us -> 18.2 us  [the longest x1 9.97 us: from_group(): lax.all_to_all(copies, BOTH, 0, 0, tiled=True, axis_index_groups=groups)]
  transfers between devices with their start and end apart: 1 -> 21, of which waited for: 1 -> 9; matrix products, arithmetic and copies ran while one was open for 7% -> 14% of each run, Pallas kernels for 0% -> 12%
where the time goes in v3:
time: 175 us; the launch traced here: 174 us
  waiting for transfers between devices  75.5 us (43%)
  starting transfers between devices  38.6 us (22%)
  Pallas kernels  29.3 us (17%)
  matrix products  13.8 us (8%)
  local copies, waits for them, and re-layouts  10.7 us (6%)
  other arithmetic  6.11 us (3%)
    ppermute x6, waiting for transfers between devices, over_x(): slabs.append(lax.ppermute(own_slab, 'pq', pairs))  22.9 us
    ppermute x7, waiting for transfers between devices, spread(): got.append(lax.ppermute(held[step], 'rs', pairs))  22.3 us
    all_to_all x1, waiting for transfers between devices, on_device(): got_far = lax.all_to_all(far, 'rs', 0, 0, tiled=True)  16.9 us
    pallas_call x2, Pallas kernels, first_product(): pl.pallas_call(functools.partial(first_kernel, groups=groups, permuted=pe...  16.5 us
    pallas_call x2, Pallas kernels, second(): pl.pallas_call(second_kernel, grid=(got.shape[2] // HALF,), in_specs=spec...  12.8 us
    all_to_all x1, starting transfers between devices, from_group(): lax.all_to_all(copies, BOTH, 0, 0, tiled=True, axis_index_groups=groups)  9.97 us
    dot_general x2, matrix products, pick(): jnp.dot(array, chosen, preferred_element_type=jnp.float32)  8.82 us
    unnamed x35, local copies, waits for them, and re-layouts  8.46 us
  transfers between devices with their start and end apart: 21, of which 9 were waited for; matrix products, arithmetic and copies ran while one was open for 14% of the time, Pallas kernels for 12%

profile of v3, /device:TPU:1, one launch (start us, length us, event | category | flops | bytes accessed | tf_op | source)
XLA Modules:
  0.0 174.3 jit_solution(7885790600639995140)
XLA Ops:
  0.0 1.4 broadcast_in_dim.34
  1.4 10.0 %all-to-all-start = ((bf16[16,36,112]{2,1,0:T(8,128)(2,1)}), bf16[16,36,112]{2,1,0:T(8,128)(2,1)S(1)}, u32[]{:S(2)}, u32[]{:S(2)}) async-start(bf16[16,36,112]{2,1,0:T(8,128)(2,1)} %broadcast_in_dim.34), calls=%async_computation | async-start | bytes 327680 | tf_op jit(solution)/shard_map/all_to_all | solution.py:37
  14.4 6.5 %all-to-all-done = bf16[16,36,112]{2,1,0:T(8,128)(2,1)S(1)} async-done(((bf16[16,36,112]{2,1,0:T(8,128)(2,1)}), bf16[16,36,112]{2,1,0:T(8,128)(2,1)S(1)}, u32[]{:S(2)}, u32[]{:S(2)}) %all-to-all-start) | async-done | bytes 129056 | tf_op jit(solution)/shard_map/all_to_all | solution.py:37
  21.3 2.8 %collective-permute-start.2 = (bf16[112,576]{1,0:T(8,128)(2,1)S(1)}, bf16[112,576]{1,0:T(8,128)(2,1)S(1)}, u32[]{:S(2)}, u32[]{:S(2)}) collective-permute-start(bf16[112,576]{1,0:T(8,128)(2,1)S(1)} %convolution_convert_fusion.3), channel_id=1, source_target_pairs={{0,24},{1,25},{2,26},{3,27},{4,28},{5,29},{6,30},{7,31},{8,16},{9,... | collective-permute-start | bytes 387080 | tf_op jit(solution)/shard_map/ppermute | solution.py:209
  24.8 5.7 %collective-permute-done.2 = bf16[112,576]{1,0:T(8,128)(2,1)S(1)} collective-permute-done((bf16[112,576]{1,0:T(8,128)(2,1)S(1)}, bf16[112,576]{1,0:T(8,128)(2,1)S(1)}, u32[]{:S(2)}, u32[]{:S(2)}) %collective-permute-start.2) | collective-permute-done | bytes 129056 | tf_op jit(solution)/shard_map/ppermute | solution.py:209
  32.0 2.6 %collective-permute-start.5 = (bf16[4,80,576]{2,1,0:T(8,128)(2,1)S(1)}, bf16[4,80,576]{2,1,0:T(8,128)(2,1)S(1)}, u32[]{:S(2)}, u32[]{:S(2)}) collective-permute-start(bf16[4,80,576]{2,1,0:T(8,128)(2,1)S(1)} %pad_maximum_fusion.1.a_ref), channel_id=1, source_target_pairs={{0,96},{32,64},{64,32},{96,0},{128,224},{160,192},{192,160},{224,1... | collective-permute-start | bytes 1105928 | tf_op jit(solution)/shard_map/ppermute | solution.py:216
  35.4 2.6 %collective-permute-start.8 = (bf16[4,32,576]{2,1,0:T(8,128)(2,1)S(1)}, bf16[4,32,576]{2,1,0:T(8,128)(2,1)S(1)}, u32[]{:S(2)}, u32[]{:S(2)}) collective-permute-start(bf16[4,32,576]{2,1,0:T(8,128)(2,1)S(1)} %pad_maximum_fusion.2.a_ref), channel_id=1, source_target_pairs={{0,96},{32,64},{64,32},{96,0},{128,224},{160,192},{192,160},{224,1... | collective-permute-start | bytes 442376 | tf_op jit(solution)/shard_map/ppermute | solution.py:216
  39.1 19.9 %collective-permute-done.8.d_ref = bf16[4,32,576]{2,1,0:T(8,128)(2,1)S(1)} collective-permute-done((bf16[4,32,576]{2,1,0:T(8,128)(2,1)S(1)}, bf16[4,32,576]{2,1,0:T(8,128)(2,1)S(1)}, u32[]{:S(2)}, u32[]{:S(2)}) %collective-permute-start.8) | collective-permute-done | bytes 147488 | tf_op jit(solution)/shard_map/ppermute | solution.py:216
  60.3 2.9 %collective-permute-done.6.b_ref = bf16[4,32,576]{2,1,0:T(8,128)(2,1)S(1)} collective-permute-done((bf16[4,32,576]{2,1,0:T(8,128)(2,1)S(1)}, bf16[4,32,576]{2,1,0:T(8,128)(2,1)S(1)}, u32[]{:S(2)}, u32[]{:S(2)}) %collective-permute-start.6) | collective-permute-done | bytes 147488 | tf_op jit(solution)/shard_map/ppermute | solution.py:216
  63.9 6.6 %shard_map.29 = (bf16[8,8,2304]{2,1,0:T(8,128)(2,1)}, bf16[8,8,2304]{2,1,0:T(8,128)(2,1)}, bf16[8,8,2304]{2,1,0:T(8,128)(2,1)}, bf16[8,8,2304]{2,1,0:T(8,128)(2,1)}, bf16[256,1152]{1,0:T(8,128)(2,1)}) custom-call(s32[1]{0:T(128)} %bitcast.own_ref, s32[1]{0:T(128)} %bitcast.1.x_ref, bf16[4,32,576]{2,1,0:T(8,128)(2,1)} %copy-done.2, ...), custom_call_target="tpu_custom_call" | custom-call | tf_op jit(solution)/shard_map/pallas_call | solution.py:102
  71.0 3.2 %collective-permute-start.11 = (bf16[8,8,2304]{2,1,0:T(8,128)(2,1)}, bf16[8,8,2304]{2,1,0:T(8,128)(2,1)}, u32[]{:S(2)}, u32[]{:S(2)}) collective-permute-start(bf16[8,8,2304]{2,1,0:T(8,128)(2,1)} %get-tuple-element.22), channel_id=1, source_target_pairs={{0,6},{1,7},{2,4},{3,5},{4,2},{5,3},{6,0},{7,1},{8,14},{9,15},{10,... | collective-permute-start | bytes 884744 | tf_op jit(solution)/shard_map/ppermute | solution.py:191
  75.7 9.8 %shard_map.28 = (bf16[32,8,5760]{2,1,0:T(8,128)(2,1)}, bf16[640,1152]{1,0:T(8,128)(2,1)}) custom-call(s32[1]{0:T(128)} %bitcast.own_ref, s32[1]{0:T(128)} %bitcast.1.x_ref, bf16[4,80,576]{2,1,0:T(8,128)(2,1)} %copy-done.1, bf16[4,80,576]{2,1,0:T(8,128)(2,1)} %copy-done.5, bf16[4,80,576]{2,1,0:T(8,128)(2,1)} %copy-done.4, bf16[4,80,576]{2,1,0:T(8,128)(2,1)} %copy-done.3, ...), custom_call_target="tpu_custom_call" | custom-call | tf_op jit(solution)/shard_map/pallas_call | solution.py:102
  85.5 8.2 %all-to-all-start.1 = ((bf16[32,8,5760]{2,1,0:T(8,128)(2,1)}), bf16[32,8,5760]{2,1,0:T(8,128)(2,1)S(1)}, u32[]{:S(2)}, u32[]{:S(2)}) async-start(bf16[32,8,5760]{2,1,0:T(8,128)(2,1)} %get-tuple-element.14), calls=%async_computation.1 | async-start | bytes 5898240 | tf_op jit(solution)/shard_map/all_to_all | solution.py:225
  93.8 4.6 %convolution_convert_fusion = bf16[1152,896]{1,0:T(8,128)(2,1)S(1)} fusion(bf16[640,1152]{1,0:T(8,128)(2,1)} %get-tuple-element.17, bf16[256,1152]{1,0:T(8,128)(2,1)} %get-tuple-element.15, s32[896]{0:T(1024)} %get-tuple-element.39, s32[896]{0:T(1024)} %get-tuple-element.40, s32[896]{0:T(1024)} %get-tuple-element.38, s32[896]{0:T(1024)} %get-tuple-element.43, ...), kind=kOutput, calls=%fused_computation.37 | convolution fusion | flops 1882144768 | bytes 4153860 | tf_op jit(solution)/shard_map/gs,gk->sk/dot_general | solution.py:233
  98.4 4.5 %convolution_convert_fusion.1.panel_ref = bf16[1152,896]{1,0:T(8,128)(2,1)} fusion(bf16[1152,896]{1,0:T(8,128)(2,1)S(1)} %convolution_convert_fusion, s32[]{:T(128)} %axis_index.22, s32[1152]{0:T(1024)S(1)} %copy-done.10, s32[1152]{0:T(1024)S(1)} %get-tuple-element.51, pred[1152]{0:T(1024)(128)(4,1)S(1)} %copy-done.13, s32[1152]{0:T(1024)S(1)} %get-tuple-element.50, ...), kind=kOutput, calls=%fused_computation.38 | convolution fusion | flops 2437595136 | bytes 4149508 | tf_op jit(solution)/shard_map/dot_general | solution.py:49
  102.9 4.4 %convolution_convert_fusion.2.panel_ref = bf16[1152,896]{1,0:T(8,128)(2,1)} fusion(bf16[1152,896]{1,0:T(8,128)(2,1)S(1)} %convolution_convert_fusion, s32[1152]{0:T(1024)S(1)} %copy-done.10, s32[1152]{0:T(1024)S(1)} %get-tuple-element.51, pred[1152]{0:T(1024)(128)(4,1)S(1)} %copy-done.13, s32[1152]{0:T(1024)S(1)} %get-tuple-element.50, ...), kind=kOutput, calls=%fused_computation.39 | convolution fusion | flops 2426978304 | bytes 4149504 | tf_op jit(solution)/shard_map/dot_general | solution.py:49
  109.7 2.6 %collective-permute-start.18 = (bf16[4,8,2304]{2,1,0:T(8,128)(2,1)S(1)}, bf16[4,8,2304]{2,1,0:T(8,128)(2,1)S(1)}, u32[]{:S(2)}, u32[]{:S(2)}) collective-permute-start(bf16[4,8,2304]{2,1,0:T(8,128)(2,1)S(1)} %get-tuple-element.23), channel_id=1, source_target_pairs={{0,25},{1,24},{2,27},{3,26},{4,29},{5,28},{6,31},{7,30},{8,17},{9,... | collective-permute-start | bytes 442376 | tf_op jit(solution)/shard_map/ppermute | solution.py:196
  112.3 2.2 %collective-permute-start.16 = (bf16[4,8,2304]{2,1,0:T(8,128)(2,1)S(1)}, bf16[4,8,2304]{2,1,0:T(8,128)(2,1)S(1)}, u32[]{:S(2)}, u32[]{:S(2)}) collective-permute-start(bf16[4,8,2304]{2,1,0:T(8,128)(2,1)S(1)} %get-tuple-element.25), channel_id=1, source_target_pairs={{0,17},{1,16},{2,19},{3,18},{4,21},{5,20},{6,23},{7,22},{8,25},{9,... | collective-permute-start | bytes 442376 | tf_op jit(solution)/shard_map/ppermute | solution.py:196
  116.7 14.8 %collective-permute-done.13 = bf16[4,8,2304]{2,1,0:T(8,128)(2,1)S(1)} collective-permute-done((bf16[4,8,2304]{2,1,0:T(8,128)(2,1)S(1)}, bf16[4,8,2304]{2,1,0:T(8,128)(2,1)S(1)}, u32[]{:S(2)}, u32[]{:S(2)}) %collective-permute-start.13) | collective-permute-done | bytes 147488 | tf_op jit(solution)/shard_map/ppermute | solution.py:196
  132.2 7.4 %collective-permute-done.14 = bf16[4,8,2304]{2,1,0:T(8,128)(2,1)S(1)} collective-permute-done((bf16[4,8,2304]{2,1,0:T(8,128)(2,1)S(1)}, bf16[4,8,2304]{2,1,0:T(8,128)(2,1)S(1)}, u32[]{:S(2)}, u32[]{:S(2)}) %collective-permute-start.14) | collective-permute-done | bytes 147488 | tf_op jit(solution)/shard_map/ppermute | solution.py:196
  143.0 4.7 %second.2.rest_0_ = bf16[28,64,896]{2,1,0:T(8,128)(2,1)} custom-call(bf16[32,8,2304]{2,1,0:T(8,128)(2,1)} %constant_dynamic-update-slice_fusion.got_ref, bf16[1152,896]{1,0:T(8,128)(2,1)} %convolution_convert_fusion.1.panel_ref), custom_call_target="tpu_custom_call" | custom-call | tf_op jit(solution)/shard_map/second/pallas_call | solution.py:158
  147.7 16.9 %all-to-all-done.1.got_ref = bf16[32,8,5760]{2,1,0:T(8,128)(2,1)S(1)} async-done(((bf16[32,8,5760]{2,1,0:T(8,128)(2,1)}), bf16[32,8,5760]{2,1,0:T(8,128)(2,1)S(1)}, u32[]{:S(2)}, u32[]{:S(2)}) %all-to-all-start.1) | async-done | bytes 2949152 | tf_op jit(solution)/shard_map/all_to_all | solution.py:225
  164.5 1.6 copy-done
  166.1 8.2 %second.3 = bf16[28,64,896]{2,1,0:T(8,128)(2,1)} custom-call(bf16[32,8,5760]{2,1,0:T(8,128)(2,1)} %copy-done, bf16[1152,896]{1,0:T(8,128)(2,1)} %convolution_convert_fusion.2.panel_ref, bf16[28,64,896]{2,1,0:T(8,128)(2,1)} %second.2.rest_0_), custom_call_target="tpu_custom_call", output_to_operand_aliasing={{}: (2, {})} | custom-call | tf_op jit(solution)/shard_map/second/pallas_call | solution.py:158
  (90 shorter events, 20.0 us)
Async XLA Ops:
  1.4 19.5 %all-to-all-start = ((bf16[16,36,112]{2,1,0:T(8,128)(2,1)}), bf16[16,36,112]{2,1,0:T(8,128)(2,1)S(1)}, u32[]{:S(2)}, u32[]{:S(2)}) async-start(bf16[16,36,112]{2,1,0:T(8,128)(2,1)} %broadcast_in_dim.34), calls=%async_computation | async-start | bytes 327680 | tf_op jit(solution)/shard_map/all_to_all | solution.py:37
  21.3 9.2 %collective-permute-start.2 = (bf16[112,576]{1,0:T(8,128)(2,1)S(1)}, bf16[112,576]{1,0:T(8,128)(2,1)S(1)}, u32[]{:S(2)}, u32[]{:S(2)}) collective-permute-start(bf16[112,576]{1,0:T(8,128)(2,1)S(1)} %convolution_convert_fusion.3), channel_id=1, source_target_pairs={{0,24},{1,25},{2,26},{3,27},{4,28},{5,29},{6,30},{7,31},{8,16},{9,... | collective-permute-start | bytes 387080 | tf_op jit(solution)/shard_map/ppermute | solution.py:209
  24.1 6.8 %collective-permute-start.1 = (bf16[112,576]{1,0:T(8,128)(2,1)S(1)}, bf16[112,576]{1,0:T(8,128)(2,1)S(1)}, u32[]{:S(2)}, u32[]{:S(2)}) collective-permute-start(bf16[112,576]{1,0:T(8,128)(2,1)S(1)} %convolution_convert_fusion.3), channel_id=1, source_target_pairs={{0,16},{1,17},{2,18},{3,19},{4,20},{5,21},{6,22},{7,23},{8,24},{9,... | collective-permute-start | bytes 387080 | tf_op jit(solution)/shard_map/ppermute | solution.py:209
  24.5 7.4 %collective-permute-start = (bf16[112,576]{1,0:T(8,128)(2,1)S(1)}, bf16[112,576]{1,0:T(8,128)(2,1)S(1)}, u32[]{:S(2)}, u32[]{:S(2)}) collective-permute-start(bf16[112,576]{1,0:T(8,128)(2,1)S(1)} %convolution_convert_fusion.3), channel_id=1, source_target_pairs={{0,8},{1,9},{2,10},{3,11},{4,12},{5,13},{6,14},{7,15},{8,0},{9,1},... | collective-permute-start | bytes 387080 | tf_op jit(solution)/shard_map/ppermute | solution.py:209
  32.0 38.6 %copy-start.1 = (bf16[4,80,576]{2,1,0:T(8,128)(2,1)}, bf16[4,80,576]{2,1,0:T(8,128)(2,1)S(1)}, u32[]{:S(2)}) copy-start(bf16[4,80,576]{2,1,0:T(8,128)(2,1)S(1)} %pad_maximum_fusion.1.a_ref) | copy-start | bytes 1105924
  32.0 39.0 %collective-permute-start.5 = (bf16[4,80,576]{2,1,0:T(8,128)(2,1)S(1)}, bf16[4,80,576]{2,1,0:T(8,128)(2,1)S(1)}, u32[]{:S(2)}, u32[]{:S(2)}) collective-permute-start(bf16[4,80,576]{2,1,0:T(8,128)(2,1)S(1)} %pad_maximum_fusion.1.a_ref), channel_id=1, source_target_pairs={{0,96},{32,64},{64,32},{96,0},{128,224},{160,192},{192,160},{224,1... | collective-permute-start | bytes 1105928 | tf_op jit(solution)/shard_map/ppermute | solution.py:216
  34.6 39.6 %collective-permute-start.4 = (bf16[4,80,576]{2,1,0:T(8,128)(2,1)S(1)}, bf16[4,80,576]{2,1,0:T(8,128)(2,1)S(1)}, u32[]{:S(2)}, u32[]{:S(2)}) collective-permute-start(bf16[4,80,576]{2,1,0:T(8,128)(2,1)S(1)} %pad_maximum_fusion.1.a_ref), channel_id=1, source_target_pairs={{0,64},{32,96},{64,0},{96,32},{128,192},{160,224},{192,128},{224,1... | collective-permute-start | bytes 1105928 | tf_op jit(solution)/shard_map/ppermute | solution.py:216
  35.1 39.1 %collective-permute-start.3 = (bf16[4,80,576]{2,1,0:T(8,128)(2,1)S(1)}, bf16[4,80,576]{2,1,0:T(8,128)(2,1)S(1)}, u32[]{:S(2)}, u32[]{:S(2)}) collective-permute-start(bf16[4,80,576]{2,1,0:T(8,128)(2,1)S(1)} %pad_maximum_fusion.1.a_ref), channel_id=1, source_target_pairs={{0,32},{32,0},{64,96},{96,64},{128,160},{160,128},{192,224},{224,1... | collective-permute-start | bytes 1105928 | tf_op jit(solution)/shard_map/ppermute | solution.py:216
  35.4 27.8 %copy-start.2 = (bf16[4,32,576]{2,1,0:T(8,128)(2,1)}, bf16[4,32,576]{2,1,0:T(8,128)(2,1)S(1)}, u32[]{:S(2)}) copy-start(bf16[4,32,576]{2,1,0:T(8,128)(2,1)S(1)} %pad_maximum_fusion.2.a_ref) | copy-start | bytes 442372
  35.4 23.6 %collective-permute-start.8 = (bf16[4,32,576]{2,1,0:T(8,128)(2,1)S(1)}, bf16[4,32,576]{2,1,0:T(8,128)(2,1)S(1)}, u32[]{:S(2)}, u32[]{:S(2)}) collective-permute-start(bf16[4,32,576]{2,1,0:T(8,128)(2,1)S(1)} %pad_maximum_fusion.2.a_ref), channel_id=1, source_target_pairs={{0,96},{32,64},{64,32},{96,0},{128,224},{160,192},{192,160},{224,1... | collective-permute-start | bytes 442376 | tf_op jit(solution)/shard_map/ppermute | solution.py:216
  38.6 21.7 %collective-permute-start.7 = (bf16[4,32,576]{2,1,0:T(8,128)(2,1)S(1)}, bf16[4,32,576]{2,1,0:T(8,128)(2,1)S(1)}, u32[]{:S(2)}, u32[]{:S(2)}) collective-permute-start(bf16[4,32,576]{2,1,0:T(8,128)(2,1)S(1)} %pad_maximum_fusion.2.a_ref), channel_id=1, source_target_pairs={{0,64},{32,96},{64,0},{96,32},{128,192},{160,224},{192,128},{224,1... | collective-permute-start | bytes 442376 | tf_op jit(solution)/shard_map/ppermute | solution.py:216
  59.0 4.2 %collective-permute-start.6 = (bf16[4,32,576]{2,1,0:T(8,128)(2,1)S(1)}, bf16[4,32,576]{2,1,0:T(8,128)(2,1)S(1)}, u32[]{:S(2)}, u32[]{:S(2)}) collective-permute-start(bf16[4,32,576]{2,1,0:T(8,128)(2,1)S(1)} %pad_maximum_fusion.2.a_ref), channel_id=1, source_target_pairs={{0,32},{32,0},{64,96},{96,64},{128,160},{160,128},{192,224},{224,1... | collective-permute-start | bytes 442376 | tf_op jit(solution)/shard_map/ppermute | solution.py:216
  70.5 36.7 %collective-permute-start.9 = (bf16[8,8,2304]{2,1,0:T(8,128)(2,1)}, bf16[8,8,2304]{2,1,0:T(8,128)(2,1)S(1)}, u32[]{:S(2)}, u32[]{:S(2)}) collective-permute-start(bf16[8,8,2304]{2,1,0:T(8,128)(2,1)} %get-tuple-element.20), channel_id=1, source_target_pairs={{0,2},{1,3},{2,0},{3,1},{4,6},{5,7},{6,4},{7,5},{8,10},{9,11},{10,... | collective-permute-start | bytes 884744 | tf_op jit(solution)/shard_map/ppermute | solution.py:191
  70.6 36.7 %collective-permute-start.10 = (bf16[8,8,2304]{2,1,0:T(8,128)(2,1)}, bf16[8,8,2304]{2,1,0:T(8,128)(2,1)S(1)}, u32[]{:S(2)}, u32[]{:S(2)}) collective-permute-start(bf16[8,8,2304]{2,1,0:T(8,128)(2,1)} %get-tuple-element.21), channel_id=1, source_target_pairs={{0,4},{1,5},{2,6},{3,7},{4,0},{5,1},{6,2},{7,3},{8,12},{9,13},{10,... | collective-permute-start | bytes 884744 | tf_op jit(solution)/shard_map/ppermute | solution.py:191
  71.0 36.3 %collective-permute-start.11 = (bf16[8,8,2304]{2,1,0:T(8,128)(2,1)}, bf16[8,8,2304]{2,1,0:T(8,128)(2,1)}, u32[]{:S(2)}, u32[]{:S(2)}) collective-permute-start(bf16[8,8,2304]{2,1,0:T(8,128)(2,1)} %get-tuple-element.22), channel_id=1, source_target_pairs={{0,6},{1,7},{2,4},{3,5},{4,2},{5,3},{6,0},{7,1},{8,14},{9,15},{10,... | collective-permute-start | bytes 884744 | tf_op jit(solution)/shard_map/ppermute | solution.py:191
  85.5 79.0 %all-to-all-start.1 = ((bf16[32,8,5760]{2,1,0:T(8,128)(2,1)}), bf16[32,8,5760]{2,1,0:T(8,128)(2,1)S(1)}, u32[]{:S(2)}, u32[]{:S(2)}) async-start(bf16[32,8,5760]{2,1,0:T(8,128)(2,1)} %get-tuple-element.14), calls=%async_computation.1 | async-start | bytes 5898240 | tf_op jit(solution)/shard_map/all_to_all | solution.py:225
  93.7 4.7 %copy-start.10 = (s32[1152]{0:T(1024)S(1)}, s32[1152]{0:T(1024)}, u32[]{:S(2)}) copy-start(s32[1152]{0:T(1024)} %get-tuple-element.48) | copy-start | bytes 13828
  108.5 7.4 %collective-permute-start.12 = (bf16[4,8,2304]{2,1,0:T(8,128)(2,1)S(1)}, bf16[4,8,2304]{2,1,0:T(8,128)(2,1)S(1)}, u32[]{:S(2)}, u32[]{:S(2)}) collective-permute-start(bf16[4,8,2304]{2,1,0:T(8,128)(2,1)S(1)} %get-tuple-element.29), channel_id=1, source_target_pairs={{0,1},{1,0},{2,3},{3,2},{4,5},{5,4},{6,7},{7,6},{8,9},{9,8},{10,11... | collective-permute-start | bytes 442376 | tf_op jit(solution)/shard_map/ppermute | solution.py:196
  109.7 32.7 %collective-permute-start.18 = (bf16[4,8,2304]{2,1,0:T(8,128)(2,1)S(1)}, bf16[4,8,2304]{2,1,0:T(8,128)(2,1)S(1)}, u32[]{:S(2)}, u32[]{:S(2)}) collective-permute-start(bf16[4,8,2304]{2,1,0:T(8,128)(2,1)S(1)} %get-tuple-element.23), channel_id=1, source_target_pairs={{0,25},{1,24},{2,27},{3,26},{4,29},{5,28},{6,31},{7,30},{8,17},{9,... | collective-permute-start | bytes 442376 | tf_op jit(solution)/shard_map/ppermute | solution.py:196
  112.2 29.4 %collective-permute-start.17 = (bf16[4,8,2304]{2,1,0:T(8,128)(2,1)S(1)}, bf16[4,8,2304]{2,1,0:T(8,128)(2,1)S(1)}, u32[]{:S(2)}, u32[]{:S(2)}) collective-permute-start(bf16[4,8,2304]{2,1,0:T(8,128)(2,1)S(1)} %get-tuple-element.24), channel_id=1, source_target_pairs={{0,24},{1,25},{2,26},{3,27},{4,28},{5,29},{6,30},{7,31},{8,16},{9,... | collective-permute-start | bytes 442376 | tf_op jit(solution)/shard_map/ppermute | solution.py:196
  112.3 28.7 %collective-permute-start.16 = (bf16[4,8,2304]{2,1,0:T(8,128)(2,1)S(1)}, bf16[4,8,2304]{2,1,0:T(8,128)(2,1)S(1)}, u32[]{:S(2)}, u32[]{:S(2)}) collective-permute-start(bf16[4,8,2304]{2,1,0:T(8,128)(2,1)S(1)} %get-tuple-element.25), channel_id=1, source_target_pairs={{0,17},{1,16},{2,19},{3,18},{4,21},{5,20},{6,23},{7,22},{8,25},{9,... | collective-permute-start | bytes 442376 | tf_op jit(solution)/shard_map/ppermute | solution.py:196
  114.5 25.8 %collective-permute-start.15 = (bf16[4,8,2304]{2,1,0:T(8,128)(2,1)S(1)}, bf16[4,8,2304]{2,1,0:T(8,128)(2,1)S(1)}, u32[]{:S(2)}, u32[]{:S(2)}) collective-permute-start(bf16[4,8,2304]{2,1,0:T(8,128)(2,1)S(1)} %get-tuple-element.26), channel_id=1, source_target_pairs={{0,16},{1,17},{2,18},{3,19},{4,20},{5,21},{6,22},{7,23},{8,24},{9,... | collective-permute-start | bytes 442376 | tf_op jit(solution)/shard_map/ppermute | solution.py:196
  115.9 15.7 %collective-permute-start.13 = (bf16[4,8,2304]{2,1,0:T(8,128)(2,1)S(1)}, bf16[4,8,2304]{2,1,0:T(8,128)(2,1)S(1)}, u32[]{:S(2)}, u32[]{:S(2)}) collective-permute-start(bf16[4,8,2304]{2,1,0:T(8,128)(2,1)S(1)} %get-tuple-element.28), channel_id=1, source_target_pairs={{0,8},{1,9},{2,10},{3,11},{4,12},{5,13},{6,14},{7,15},{8,0},{9,1},... | collective-permute-start | bytes 442376 | tf_op jit(solution)/shard_map/ppermute | solution.py:196
  131.6 8.1 %collective-permute-start.14 = (bf16[4,8,2304]{2,1,0:T(8,128)(2,1)S(1)}, bf16[4,8,2304]{2,1,0:T(8,128)(2,1)S(1)}, u32[]{:S(2)}, u32[]{:S(2)}) collective-permute-start(bf16[4,8,2304]{2,1,0:T(8,128)(2,1)S(1)} %get-tuple-element.27), channel_id=1, source_target_pairs={{0,9},{1,8},{2,11},{3,10},{4,13},{5,12},{6,15},{7,14},{8,1},{9,0},... | collective-permute-start | bytes 442376 | tf_op jit(solution)/shard_map/ppermute | solution.py:196
  (11 other events, 32.4 us)

commit v4 on v3

--- a/solution.py
+++ b/solution.py
@@ -18,6 +18,7 @@
 LANES = ROWS * PAIRS
 SOON, FAR = 2, 5
 HALF = LANES // 2
+ALL_VMEM = 63 * 2**20
 BOTH = ("pq", "rs")
 
 
@@ -111,6 +112,7 @@
         out_specs=[whole(shape) for shape in shapes],
         out_shape=[jax.ShapeDtypeStruct(shape, jnp.bfloat16) for shape in shapes],
         scratch_shapes=[pltpu.VMEM((NBASIS, groups * 128), jnp.bfloat16)],
+        compiler_params=pltpu.CompilerParams(vmem_limit_bytes=ALL_VMEM),
     )(own.reshape(1), x.reshape(1), *slabs, flat, flat)
 
 
@@ -166,6 +168,7 @@
             pltpu.VMEM((4 * PAIRS, NBASIS), jnp.bfloat16),
         ],
         input_output_aliases=aliases,
+        compiler_params=pltpu.CompilerParams(vmem_limit_bytes=ALL_VMEM),
         name="second",
     )(*operands)
 
@@ -203,21 +206,21 @@
     flat = integrals.transpose(1, 0, 2).reshape(LANES, NBASIS)
 
     strip = from_group(coeff, ALONG_Z).reshape(2, 8 * ROWS, WIDTH)
-    columns = columns_of(0, SOON + FAR, strip)
-    slab = [columns]
-    for step in (1, 2, 3):
-        slab.append(lax.ppermute(columns, "rs", [(j, j ^ step * 8) for j in range(COUNT)]))
-
-    def over_x(lo, hi):
-        own_slab = jnp.stack([part[lo * 16 : hi * 16] for part in slab])
-        slabs = [own_slab]
+
+    def gathered(first, groups):
+        columns = columns_of(first, groups, strip)
+        slab = [columns]
+        for step in (1, 2, 3):
+            slab.append(lax.ppermute(columns, "rs", [(j, j ^ step * 8) for j in range(COUNT)]))
+        slab = jnp.stack(slab)
+        slabs = [slab]
         for step in (1, 2, 3):
             pairs = [(i, i & 4 | (i & 3) ^ step) for i in range(8)]
-            slabs.append(lax.ppermute(own_slab, "pq", pairs))
+            slabs.append(lax.ppermute(slab, "pq", pairs))
         return slabs
 
-    early = over_x(0, SOON)
-    late = over_x(SOON, SOON + FAR)
+    early = gathered(0, SOON)
+    late = gathered(SOON, FAR)
     *soon, soon_part = first_product(early, flat, own, x, True)
     far, far_part = first_product(late, flat, own, x, False)
 

time: 175 us -> 169 us (0.966)
  waiting for transfers between devices: 75.5 us -> 64.6 us
  starting transfers between devices: 38.6 us -> 47.1 us
  local copies, waits for them, and re-layouts: 10.7 us -> 8.25 us
    ppermute x9 -> x12, waiting for transfers between devices: 29.9 us -> 18 us  [the longest x6 16.3 us: gathered(): slabs.append(lax.ppermute(slab, 'pq', pairs))]
    ppermute x9 -> x12, starting transfers between devices: 9.93 us -> 15.8 us  [the longest x6 8.96 us: gathered(): slabs.append(lax.ppermute(slab, 'pq', pairs))]
    all_to_all x1, starting transfers between devices: 8.23 us -> 10.8 us  [on_device(): got_far = lax.all_to_all(far, 'rs', 0, 0, tiled=True)]
    unnamed x35 -> x57, local copies, waits for them, and re-layouts: 8.46 us -> 6.08 us
  transfers between devices with their start and end apart: 21 -> 24, of which waited for: 9 -> 8; matrix products, arithmetic and copies ran while one was open for 14% -> 14% of each run, Pallas kernels for 12% -> 13%
where the time goes in v4:
time: 169 us
  waiting for transfers between devices  64.6 us (38%)
  starting transfers between devices  47.1 us (28%)
  Pallas kernels  29.4 us (17%)
  matrix products  12.4 us (7%)
  local copies, waits for them, and re-layouts  8.25 us (5%)
  other arithmetic  6.81 us (4%)
    ppermute x7, waiting for transfers between devices, spread(): got.append(lax.ppermute(held[step], 'rs', pairs))  23.6 us
    pallas_call x2, Pallas kernels, first_product(): pl.pallas_call(functools.partial(first_kernel, groups=groups, permuted=pe...  16.5 us
    all_to_all x1, waiting for transfers between devices, on_device(): got_far = lax.all_to_all(far, 'rs', 0, 0, tiled=True)  16.5 us
    ppermute x6, waiting for transfers between devices, gathered(): slabs.append(lax.ppermute(slab, 'pq', pairs))  16.3 us
    pallas_call x2, Pallas kernels, second(): pl.pallas_call(second_kernel, grid=(got.shape[2] // HALF,), in_specs=spec...  12.9 us
    all_to_all x1, starting transfers between devices, on_device(): got_far = lax.all_to_all(far, 'rs', 0, 0, tiled=True)  10.8 us
    all_to_all x1, starting transfers between devices, from_group(): lax.all_to_all(copies, BOTH, 0, 0, tiled=True, axis_index_groups=groups)  9.97 us
    ppermute x6, starting transfers between devices, gathered(): slabs.append(lax.ppermute(slab, 'pq', pairs))  8.96 us
  transfers between devices with their start and end apart: 24, of which 8 were waited for; matrix products, arithmetic and copies ran while one was open for 14% of the time, Pallas kernels for 13%

profile of v4, /device:TPU:1, one launch (start us, length us, event | category | flops | bytes accessed | tf_op | source)
XLA Modules:
  0.0 169.0 jit_solution(572203275481907347)
XLA Ops:
  0.0 1.4 broadcast_in_dim.42
  1.4 10.0 %all-to-all-start = ((bf16[16,36,112]{2,1,0:T(8,128)(2,1)}), bf16[16,36,112]{2,1,0:T(8,128)(2,1)S(1)}, u32[]{:S(2)}, u32[]{:S(2)}) async-start(bf16[16,36,112]{2,1,0:T(8,128)(2,1)} %broadcast_in_dim.42), calls=%async_computation | async-start | bytes 327680 | tf_op jit(solution)/shard_map/all_to_all | solution.py:38
  14.4 6.4 %all-to-all-done = bf16[16,36,112]{2,1,0:T(8,128)(2,1)S(1)} async-done(((bf16[16,36,112]{2,1,0:T(8,128)(2,1)}), bf16[16,36,112]{2,1,0:T(8,128)(2,1)S(1)}, u32[]{:S(2)}, u32[]{:S(2)}) %all-to-all-start) | async-done | bytes 129056 | tf_op jit(solution)/shard_map/all_to_all | solution.py:38
  21.2 2.8 %collective-permute-start.8 = (bf16[32,576]{1,0:T(8,128)(2,1)S(1)}, bf16[32,576]{1,0:T(8,128)(2,1)S(1)}, u32[]{:S(2)}, u32[]{:S(2)}) collective-permute-start(bf16[32,576]{1,0:T(8,128)(2,1)S(1)} %convolution_convert_fusion.4), channel_id=1, source_target_pairs={{0,24},{1,25},{2,26},{3,27},{4,28},{5,29},{6,30},{7,31},{8,16},{9,... | collective-permute-start | bytes 110600 | tf_op jit(solution)/shard_map/ppermute | solution.py:214
  24.9 2.7 %collective-permute-start.2 = (bf16[80,576]{1,0:T(8,128)(2,1)S(1)}, bf16[80,576]{1,0:T(8,128)(2,1)S(1)}, u32[]{:S(2)}, u32[]{:S(2)}) collective-permute-start(bf16[80,576]{1,0:T(8,128)(2,1)S(1)} %convolution_convert_fusion.3), channel_id=1, source_target_pairs={{0,24},{1,25},{2,26},{3,27},{4,28},{5,29},{6,30},{7,31},{8,16},{9,... | collective-permute-start | bytes 276488 | tf_op jit(solution)/shard_map/ppermute | solution.py:214
  28.4 2.6 %collective-permute-start.11 = (bf16[4,32,576]{2,1,0:T(8,128)(2,1)S(1)}, bf16[4,32,576]{2,1,0:T(8,128)(2,1)S(1)}, u32[]{:S(2)}, u32[]{:S(2)}) collective-permute-start(bf16[4,32,576]{2,1,0:T(8,128)(2,1)S(1)} %pad_maximum_fusion.2.a_ref), channel_id=1, source_target_pairs={{0,96},{32,64},{64,32},{96,0},{128,224},{160,192},{192,160},{224,1... | collective-permute-start | bytes 442376 | tf_op jit(solution)/shard_map/ppermute | solution.py:219
  32.7 2.6 %collective-permute-start.5 = (bf16[4,80,576]{2,1,0:T(8,128)(2,1)S(1)}, bf16[4,80,576]{2,1,0:T(8,128)(2,1)S(1)}, u32[]{:S(2)}, u32[]{:S(2)}) collective-permute-start(bf16[4,80,576]{2,1,0:T(8,128)(2,1)S(1)} %pad_maximum_fusion.1.a_ref), channel_id=1, source_target_pairs={{0,96},{32,64},{64,32},{96,0},{128,224},{160,192},{192,160},{224,1... | collective-permute-start | bytes 1105928 | tf_op jit(solution)/shard_map/ppermute | solution.py:219
  37.3 2.7 %collective-permute-start.10 = (bf16[4,32,576]{2,1,0:T(8,128)(2,1)S(1)}, bf16[4,32,576]{2,1,0:T(8,128)(2,1)S(1)}, u32[]{:S(2)}, u32[]{:S(2)}) collective-permute-start(bf16[4,32,576]{2,1,0:T(8,128)(2,1)S(1)} %pad_maximum_fusion.2.a_ref), channel_id=1, source_target_pairs={{0,64},{32,96},{64,0},{96,32},{128,192},{160,224},{192,128},{224,1... | collective-permute-start | bytes 442376 | tf_op jit(solution)/shard_map/ppermute | solution.py:219
  42.2 14.6 %collective-permute-done.10.c_ref = bf16[4,32,576]{2,1,0:T(8,128)(2,1)S(1)} collective-permute-done((bf16[4,32,576]{2,1,0:T(8,128)(2,1)S(1)}, bf16[4,32,576]{2,1,0:T(8,128)(2,1)S(1)}, u32[]{:S(2)}, u32[]{:S(2)}) %collective-permute-start.10) | collective-permute-done | bytes 147488 | tf_op jit(solution)/shard_map/ppermute | solution.py:219
  56.7 1.7 %collective-permute-done.9.b_ref = bf16[4,32,576]{2,1,0:T(8,128)(2,1)S(1)} collective-permute-done((bf16[4,32,576]{2,1,0:T(8,128)(2,1)S(1)}, bf16[4,32,576]{2,1,0:T(8,128)(2,1)S(1)}, u32[]{:S(2)}, u32[]{:S(2)}) %collective-permute-start.9) | collective-permute-done | bytes 147488 | tf_op jit(solution)/shard_map/ppermute | solution.py:219
  59.1 6.6 %shard_map.29 = (bf16[8,8,2304]{2,1,0:T(8,128)(2,1)}, bf16[8,8,2304]{2,1,0:T(8,128)(2,1)}, bf16[8,8,2304]{2,1,0:T(8,128)(2,1)}, bf16[8,8,2304]{2,1,0:T(8,128)(2,1)}, bf16[256,1152]{1,0:T(8,128)(2,1)}) custom-call(s32[1]{0:T(128)} %bitcast.own_ref, s32[1]{0:T(128)} %bitcast.1.x_ref, bf16[4,32,576]{2,1,0:T(8,128)(2,1)} %copy-done.1, ...), custom_call_target="tpu_custom_call" | custom-call | tf_op jit(solution)/shard_map/pallas_call | solution.py:103
  66.8 2.6 %collective-permute-start.14 = (bf16[8,8,2304]{2,1,0:T(8,128)(2,1)}, bf16[8,8,2304]{2,1,0:T(8,128)(2,1)}, u32[]{:S(2)}, u32[]{:S(2)}) collective-permute-start(bf16[8,8,2304]{2,1,0:T(8,128)(2,1)} %get-tuple-element.22), channel_id=1, source_target_pairs={{0,6},{1,7},{2,4},{3,5},{4,2},{5,3},{6,0},{7,1},{8,14},{9,15},{10,... | collective-permute-start | bytes 884744 | tf_op jit(solution)/shard_map/ppermute | solution.py:194
  69.4 9.9 %shard_map.28 = (bf16[32,8,5760]{2,1,0:T(8,128)(2,1)}, bf16[640,1152]{1,0:T(8,128)(2,1)}) custom-call(s32[1]{0:T(128)} %bitcast.own_ref, s32[1]{0:T(128)} %bitcast.1.x_ref, bf16[4,80,576]{2,1,0:T(8,128)(2,1)} %copy-done, bf16[4,80,576]{2,1,0:T(8,128)(2,1)} %collective-permute-done.3.b_ref, bf16[4,80,576]{2,1,0:T(8,128)(2,1)} %collective-permute-done.4.c_ref, ...), custom_call_target="tpu_custom_call" | custom-call | tf_op jit(solution)/shard_map/pallas_call | solution.py:103
  79.3 10.8 %all-to-all-start.1 = ((bf16[32,8,5760]{2,1,0:T(8,128)(2,1)}), bf16[32,8,5760]{2,1,0:T(8,128)(2,1)}, u32[]{:S(2)}, u32[]{:S(2)}) async-start(bf16[32,8,5760]{2,1,0:T(8,128)(2,1)} %get-tuple-element.14), calls=%async_computation.1 | async-start | bytes 5898240 | tf_op jit(solution)/shard_map/all_to_all | solution.py:228
  90.4 3.0 %convolution_convert_fusion = bf16[1152,896]{1,0:T(8,128)(2,1)S(1)} fusion(bf16[640,1152]{1,0:T(8,128)(2,1)S(1)} %copy-done.23, bf16[256,1152]{1,0:T(8,128)(2,1)S(1)} %copy-done.24, s32[896]{0:T(1024)S(1)} %copy-done.16, s32[896]{0:T(1024)S(1)} %copy-done.13, s32[896]{0:T(1024)S(1)} %copy-done.15, s32[896]{0:T(1024)S(1)} %copy-done.12, s32[]{:T(128)} %axis_index.22, ...), kind=kOutput, calls=%fused_computation.37 | convolution fusion | flops 1882144768 | bytes 4153860 | tf_op jit(solution)/shard_map/gs,gk->sk/dot_general | solution.py:236
  93.5 4.5 %convolution_convert_fusion.1.panel_ref = bf16[1152,896]{1,0:T(8,128)(2,1)} fusion(bf16[1152,896]{1,0:T(8,128)(2,1)S(1)} %convolution_convert_fusion, s32[]{:T(128)} %axis_index.22, s32[1152]{0:T(1024)S(1)} %copy-done.9, s32[1152]{0:T(1024)S(1)} %copy-done.8, pred[1152]{0:T(1024)(128)(4,1)S(1)} %copy-done.18, s32[1152]{0:T(1024)S(1)} %copy-done.7, ...), kind=kOutput, calls=%fused_computation.38 | convolution fusion | flops 2437595136 | bytes 4149508 | tf_op jit(solution)/shard_map/dot_general | solution.py:50
  98.0 4.4 %convolution_convert_fusion.2.panel_ref = bf16[1152,896]{1,0:T(8,128)(2,1)} fusion(bf16[1152,896]{1,0:T(8,128)(2,1)S(1)} %convolution_convert_fusion, s32[1152]{0:T(1024)S(1)} %copy-done.9, s32[1152]{0:T(1024)S(1)} %copy-done.8, pred[1152]{0:T(1024)(128)(4,1)S(1)} %copy-done.18, s32[1152]{0:T(1024)S(1)} %copy-done.7, s32[1152]{0:T(1024)S(1)} %copy-done.10, ...), kind=kOutput, calls=%fused_computation.39 | convolution fusion | flops 2426978304 | bytes 4149504 | tf_op jit(solution)/shard_map/dot_general | solution.py:50
  104.8 2.7 %collective-permute-start.21 = (bf16[4,8,2304]{2,1,0:T(8,128)(2,1)S(1)}, bf16[4,8,2304]{2,1,0:T(8,128)(2,1)S(1)}, u32[]{:S(2)}, u32[]{:S(2)}) collective-permute-start(bf16[4,8,2304]{2,1,0:T(8,128)(2,1)S(1)} %get-tuple-element.23), channel_id=1, source_target_pairs={{0,25},{1,24},{2,27},{3,26},{4,29},{5,28},{6,31},{7,30},{8,17},{9,... | collective-permute-start | bytes 442376 | tf_op jit(solution)/shard_map/ppermute | solution.py:199
  107.6 2.2 %collective-permute-start.19 = (bf16[4,8,2304]{2,1,0:T(8,128)(2,1)S(1)}, bf16[4,8,2304]{2,1,0:T(8,128)(2,1)S(1)}, u32[]{:S(2)}, u32[]{:S(2)}) collective-permute-start(bf16[4,8,2304]{2,1,0:T(8,128)(2,1)S(1)} %get-tuple-element.25), channel_id=1, source_target_pairs={{0,17},{1,16},{2,19},{3,18},{4,21},{5,20},{6,23},{7,22},{8,25},{9,... | collective-permute-start | bytes 442376 | tf_op jit(solution)/shard_map/ppermute | solution.py:199
  112.0 16.2 %collective-permute-done.16 = bf16[4,8,2304]{2,1,0:T(8,128)(2,1)S(1)} collective-permute-done((bf16[4,8,2304]{2,1,0:T(8,128)(2,1)S(1)}, bf16[4,8,2304]{2,1,0:T(8,128)(2,1)S(1)}, u32[]{:S(2)}, u32[]{:S(2)}) %collective-permute-start.16) | collective-permute-done | bytes 147488 | tf_op jit(solution)/shard_map/ppermute | solution.py:199
  128.8 7.5 %collective-permute-done.17 = bf16[4,8,2304]{2,1,0:T(8,128)(2,1)S(1)} collective-permute-done((bf16[4,8,2304]{2,1,0:T(8,128)(2,1)S(1)}, bf16[4,8,2304]{2,1,0:T(8,128)(2,1)S(1)}, u32[]{:S(2)}, u32[]{:S(2)}) %collective-permute-start.17) | collective-permute-done | bytes 147488 | tf_op jit(solution)/shard_map/ppermute | solution.py:199
  139.6 4.7 %second.2.rest_0_ = bf16[28,64,896]{2,1,0:T(8,128)(2,1)} custom-call(bf16[32,8,2304]{2,1,0:T(8,128)(2,1)} %constant_dynamic-update-slice_fusion.got_ref, bf16[1152,896]{1,0:T(8,128)(2,1)} %convolution_convert_fusion.1.panel_ref), custom_call_target="tpu_custom_call" | custom-call | tf_op jit(solution)/shard_map/second/pallas_call | solution.py:160
  144.3 16.5 %all-to-all-done.1.got_ref = bf16[32,8,5760]{2,1,0:T(8,128)(2,1)} async-done(((bf16[32,8,5760]{2,1,0:T(8,128)(2,1)}), bf16[32,8,5760]{2,1,0:T(8,128)(2,1)}, u32[]{:S(2)}, u32[]{:S(2)}) %all-to-all-start.1) | async-done | bytes 2949152 | tf_op jit(solution)/shard_map/all_to_all | solution.py:228
  160.8 8.2 %second.3 = bf16[28,64,896]{2,1,0:T(8,128)(2,1)} custom-call(bf16[32,8,5760]{2,1,0:T(8,128)(2,1)} %all-to-all-done.1.got_ref, bf16[1152,896]{1,0:T(8,128)(2,1)} %convolution_convert_fusion.2.panel_ref, bf16[28,64,896]{2,1,0:T(8,128)(2,1)} %second.2.rest_0_), custom_call_target="tpu_custom_call", output_to_operand_aliasing={{}: (2, {})} | custom-call | tf_op jit(solution)/shard_map/second/pallas_call | solution.py:160
  (116 shorter events, 21.4 us)
Async XLA Ops:
  1.4 19.5 %all-to-all-start = ((bf16[16,36,112]{2,1,0:T(8,128)(2,1)}), bf16[16,36,112]{2,1,0:T(8,128)(2,1)S(1)}, u32[]{:S(2)}, u32[]{:S(2)}) async-start(bf16[16,36,112]{2,1,0:T(8,128)(2,1)} %broadcast_in_dim.42), calls=%async_computation | async-start | bytes 327680 | tf_op jit(solution)/shard_map/all_to_all | solution.py:38
  21.2 6.8 %collective-permute-start.8 = (bf16[32,576]{1,0:T(8,128)(2,1)S(1)}, bf16[32,576]{1,0:T(8,128)(2,1)S(1)}, u32[]{:S(2)}, u32[]{:S(2)}) collective-permute-start(bf16[32,576]{1,0:T(8,128)(2,1)S(1)} %convolution_convert_fusion.4), channel_id=1, source_target_pairs={{0,24},{1,25},{2,26},{3,27},{4,28},{5,29},{6,30},{7,31},{8,16},{9,... | collective-permute-start | bytes 110600 | tf_op jit(solution)/shard_map/ppermute | solution.py:214
  24.0 4.4 %collective-permute-start.7 = (bf16[32,576]{1,0:T(8,128)(2,1)S(1)}, bf16[32,576]{1,0:T(8,128)(2,1)S(1)}, u32[]{:S(2)}, u32[]{:S(2)}) collective-permute-start(bf16[32,576]{1,0:T(8,128)(2,1)S(1)} %convolution_convert_fusion.4), channel_id=1, source_target_pairs={{0,16},{1,17},{2,18},{3,19},{4,20},{5,21},{6,22},{7,23},{8,24},{9,... | collective-permute-start | bytes 110600 | tf_op jit(solution)/shard_map/ppermute | solution.py:214
  24.3 4.0 %collective-permute-start.6 = (bf16[32,576]{1,0:T(8,128)(2,1)S(1)}, bf16[32,576]{1,0:T(8,128)(2,1)S(1)}, u32[]{:S(2)}, u32[]{:S(2)}) collective-permute-start(bf16[32,576]{1,0:T(8,128)(2,1)S(1)} %convolution_convert_fusion.4), channel_id=1, source_target_pairs={{0,8},{1,9},{2,10},{3,11},{4,12},{5,13},{6,14},{7,15},{8,0},{9,1},... | collective-permute-start | bytes 110600 | tf_op jit(solution)/shard_map/ppermute | solution.py:214
  24.9 6.7 %collective-permute-start.2 = (bf16[80,576]{1,0:T(8,128)(2,1)S(1)}, bf16[80,576]{1,0:T(8,128)(2,1)S(1)}, u32[]{:S(2)}, u32[]{:S(2)}) collective-permute-start(bf16[80,576]{1,0:T(8,128)(2,1)S(1)} %convolution_convert_fusion.3), channel_id=1, source_target_pairs={{0,24},{1,25},{2,26},{3,27},{4,28},{5,29},{6,30},{7,31},{8,16},{9,... | collective-permute-start | bytes 276488 | tf_op jit(solution)/shard_map/ppermute | solution.py:214
  27.6 5.0 %collective-permute-start.1 = (bf16[80,576]{1,0:T(8,128)(2,1)S(1)}, bf16[80,576]{1,0:T(8,128)(2,1)S(1)}, u32[]{:S(2)}, u32[]{:S(2)}) collective-permute-start(bf16[80,576]{1,0:T(8,128)(2,1)S(1)} %convolution_convert_fusion.3), channel_id=1, source_target_pairs={{0,16},{1,17},{2,18},{3,19},{4,20},{5,21},{6,22},{7,23},{8,24},{9,... | collective-permute-start | bytes 276488 | tf_op jit(solution)/shard_map/ppermute | solution.py:214
  28.0 4.7 %collective-permute-start = (bf16[80,576]{1,0:T(8,128)(2,1)S(1)}, bf16[80,576]{1,0:T(8,128)(2,1)S(1)}, u32[]{:S(2)}, u32[]{:S(2)}) collective-permute-start(bf16[80,576]{1,0:T(8,128)(2,1)S(1)} %convolution_convert_fusion.3), channel_id=1, source_target_pairs={{0,8},{1,9},{2,10},{3,11},{4,12},{5,13},{6,14},{7,15},{8,0},{9,1},... | collective-permute-start | bytes 276488 | tf_op jit(solution)/shard_map/ppermute | solution.py:214
  28.4 11.6 %collective-permute-start.11 = (bf16[4,32,576]{2,1,0:T(8,128)(2,1)S(1)}, bf16[4,32,576]{2,1,0:T(8,128)(2,1)S(1)}, u32[]{:S(2)}, u32[]{:S(2)}) collective-permute-start(bf16[4,32,576]{2,1,0:T(8,128)(2,1)S(1)} %pad_maximum_fusion.2.a_ref), channel_id=1, source_target_pairs={{0,96},{32,64},{64,32},{96,0},{128,224},{160,192},{192,160},{224,1... | collective-permute-start | bytes 442376 | tf_op jit(solution)/shard_map/ppermute | solution.py:219
  32.7 34.1 %collective-permute-start.5 = (bf16[4,80,576]{2,1,0:T(8,128)(2,1)S(1)}, bf16[4,80,576]{2,1,0:T(8,128)(2,1)S(1)}, u32[]{:S(2)}, u32[]{:S(2)}) collective-permute-start(bf16[4,80,576]{2,1,0:T(8,128)(2,1)S(1)} %pad_maximum_fusion.1.a_ref), channel_id=1, source_target_pairs={{0,96},{32,64},{64,32},{96,0},{128,224},{160,192},{192,160},{224,1... | collective-permute-start | bytes 1105928 | tf_op jit(solution)/shard_map/ppermute | solution.py:219
  35.3 34.1 %collective-permute-start.4 = (bf16[4,80,576]{2,1,0:T(8,128)(2,1)S(1)}, bf16[4,80,576]{2,1,0:T(8,128)(2,1)}, u32[]{:S(2)}, u32[]{:S(2)}) collective-permute-start(bf16[4,80,576]{2,1,0:T(8,128)(2,1)S(1)} %pad_maximum_fusion.1.a_ref), channel_id=1, source_target_pairs={{0,64},{32,96},{64,0},{96,32},{128,192},{160,224},{192,128},{224,1... | collective-permute-start | bytes 1105928 | tf_op jit(solution)/shard_map/ppermute | solution.py:219
  35.8 33.6 %collective-permute-start.3 = (bf16[4,80,576]{2,1,0:T(8,128)(2,1)S(1)}, bf16[4,80,576]{2,1,0:T(8,128)(2,1)}, u32[]{:S(2)}, u32[]{:S(2)}) collective-permute-start(bf16[4,80,576]{2,1,0:T(8,128)(2,1)S(1)} %pad_maximum_fusion.1.a_ref), channel_id=1, source_target_pairs={{0,32},{32,0},{64,96},{96,64},{128,160},{160,128},{192,224},{224,1... | collective-permute-start | bytes 1105928 | tf_op jit(solution)/shard_map/ppermute | solution.py:219
  37.3 19.5 %collective-permute-start.10 = (bf16[4,32,576]{2,1,0:T(8,128)(2,1)S(1)}, bf16[4,32,576]{2,1,0:T(8,128)(2,1)S(1)}, u32[]{:S(2)}, u32[]{:S(2)}) collective-permute-start(bf16[4,32,576]{2,1,0:T(8,128)(2,1)S(1)} %pad_maximum_fusion.2.a_ref), channel_id=1, source_target_pairs={{0,64},{32,96},{64,0},{96,32},{128,192},{160,224},{192,128},{224,1... | collective-permute-start | bytes 442376 | tf_op jit(solution)/shard_map/ppermute | solution.py:219
  40.7 17.8 %collective-permute-start.9 = (bf16[4,32,576]{2,1,0:T(8,128)(2,1)S(1)}, bf16[4,32,576]{2,1,0:T(8,128)(2,1)S(1)}, u32[]{:S(2)}, u32[]{:S(2)}) collective-permute-start(bf16[4,32,576]{2,1,0:T(8,128)(2,1)S(1)} %pad_maximum_fusion.2.a_ref), channel_id=1, source_target_pairs={{0,32},{32,0},{64,96},{96,64},{128,160},{160,128},{192,224},{224,1... | collective-permute-start | bytes 442376 | tf_op jit(solution)/shard_map/ppermute | solution.py:219
  65.8 36.6 %collective-permute-start.12 = (bf16[8,8,2304]{2,1,0:T(8,128)(2,1)}, bf16[8,8,2304]{2,1,0:T(8,128)(2,1)}, u32[]{:S(2)}, u32[]{:S(2)}) collective-permute-start(bf16[8,8,2304]{2,1,0:T(8,128)(2,1)} %get-tuple-element.20), channel_id=1, source_target_pairs={{0,2},{1,3},{2,0},{3,1},{4,6},{5,7},{6,4},{7,5},{8,10},{9,11},{10,... | collective-permute-start | bytes 884744 | tf_op jit(solution)/shard_map/ppermute | solution.py:194
  66.0 36.4 %collective-permute-start.13 = (bf16[8,8,2304]{2,1,0:T(8,128)(2,1)}, bf16[8,8,2304]{2,1,0:T(8,128)(2,1)}, u32[]{:S(2)}, u32[]{:S(2)}) collective-permute-start(bf16[8,8,2304]{2,1,0:T(8,128)(2,1)} %get-tuple-element.21), channel_id=1, source_target_pairs={{0,4},{1,5},{2,6},{3,7},{4,0},{5,1},{6,2},{7,3},{8,12},{9,13},{10,... | collective-permute-start | bytes 884744 | tf_op jit(solution)/shard_map/ppermute | solution.py:194
  66.8 35.6 %collective-permute-start.14 = (bf16[8,8,2304]{2,1,0:T(8,128)(2,1)}, bf16[8,8,2304]{2,1,0:T(8,128)(2,1)}, u32[]{:S(2)}, u32[]{:S(2)}) collective-permute-start(bf16[8,8,2304]{2,1,0:T(8,128)(2,1)} %get-tuple-element.22), channel_id=1, source_target_pairs={{0,6},{1,7},{2,4},{3,5},{4,2},{5,3},{6,0},{7,1},{8,14},{9,15},{10,... | collective-permute-start | bytes 884744 | tf_op jit(solution)/shard_map/ppermute | solution.py:194
  79.3 81.4 %all-to-all-start.1 = ((bf16[32,8,5760]{2,1,0:T(8,128)(2,1)}), bf16[32,8,5760]{2,1,0:T(8,128)(2,1)}, u32[]{:S(2)}, u32[]{:S(2)}) async-start(bf16[32,8,5760]{2,1,0:T(8,128)(2,1)} %get-tuple-element.14), calls=%async_computation.1 | async-start | bytes 5898240 | tf_op jit(solution)/shard_map/all_to_all | solution.py:228
  103.8 7.3 %collective-permute-start.15 = (bf16[4,8,2304]{2,1,0:T(8,128)(2,1)S(1)}, bf16[4,8,2304]{2,1,0:T(8,128)(2,1)S(1)}, u32[]{:S(2)}, u32[]{:S(2)}) collective-permute-start(bf16[4,8,2304]{2,1,0:T(8,128)(2,1)S(1)} %get-tuple-element.29), channel_id=1, source_target_pairs={{0,1},{1,0},{2,3},{3,2},{4,5},{5,4},{6,7},{7,6},{8,9},{9,8},{10,11... | collective-permute-start | bytes 442376 | tf_op jit(solution)/shard_map/ppermute | solution.py:199
  104.8 34.2 %collective-permute-start.21 = (bf16[4,8,2304]{2,1,0:T(8,128)(2,1)S(1)}, bf16[4,8,2304]{2,1,0:T(8,128)(2,1)S(1)}, u32[]{:S(2)}, u32[]{:S(2)}) collective-permute-start(bf16[4,8,2304]{2,1,0:T(8,128)(2,1)S(1)} %get-tuple-element.23), channel_id=1, source_target_pairs={{0,25},{1,24},{2,27},{3,26},{4,29},{5,28},{6,31},{7,30},{8,17},{9,... | collective-permute-start | bytes 442376 | tf_op jit(solution)/shard_map/ppermute | solution.py:199
  107.5 30.8 %collective-permute-start.20 = (bf16[4,8,2304]{2,1,0:T(8,128)(2,1)S(1)}, bf16[4,8,2304]{2,1,0:T(8,128)(2,1)S(1)}, u32[]{:S(2)}, u32[]{:S(2)}) collective-permute-start(bf16[4,8,2304]{2,1,0:T(8,128)(2,1)S(1)} %get-tuple-element.24), channel_id=1, source_target_pairs={{0,24},{1,25},{2,26},{3,27},{4,28},{5,29},{6,30},{7,31},{8,16},{9,... | collective-permute-start | bytes 442376 | tf_op jit(solution)/shard_map/ppermute | solution.py:199
  107.6 30.0 %collective-permute-start.19 = (bf16[4,8,2304]{2,1,0:T(8,128)(2,1)S(1)}, bf16[4,8,2304]{2,1,0:T(8,128)(2,1)S(1)}, u32[]{:S(2)}, u32[]{:S(2)}) collective-permute-start(bf16[4,8,2304]{2,1,0:T(8,128)(2,1)S(1)} %get-tuple-element.25), channel_id=1, source_target_pairs={{0,17},{1,16},{2,19},{3,18},{4,21},{5,20},{6,23},{7,22},{8,25},{9,... | collective-permute-start | bytes 442376 | tf_op jit(solution)/shard_map/ppermute | solution.py:199
  109.8 27.2 %collective-permute-start.18 = (bf16[4,8,2304]{2,1,0:T(8,128)(2,1)S(1)}, bf16[4,8,2304]{2,1,0:T(8,128)(2,1)S(1)}, u32[]{:S(2)}, u32[]{:S(2)}) collective-permute-start(bf16[4,8,2304]{2,1,0:T(8,128)(2,1)S(1)} %get-tuple-element.26), channel_id=1, source_target_pairs={{0,16},{1,17},{2,18},{3,19},{4,20},{5,21},{6,22},{7,23},{8,24},{9,... | collective-permute-start | bytes 442376 | tf_op jit(solution)/shard_map/ppermute | solution.py:199
  111.0 17.2 %collective-permute-start.16 = (bf16[4,8,2304]{2,1,0:T(8,128)(2,1)S(1)}, bf16[4,8,2304]{2,1,0:T(8,128)(2,1)S(1)}, u32[]{:S(2)}, u32[]{:S(2)}) collective-permute-start(bf16[4,8,2304]{2,1,0:T(8,128)(2,1)S(1)} %get-tuple-element.28), channel_id=1, source_target_pairs={{0,8},{1,9},{2,10},{3,11},{4,12},{5,13},{6,14},{7,15},{8,0},{9,1},... | collective-permute-start | bytes 442376 | tf_op jit(solution)/shard_map/ppermute | solution.py:199
  128.2 8.1 %collective-permute-start.17 = (bf16[4,8,2304]{2,1,0:T(8,128)(2,1)S(1)}, bf16[4,8,2304]{2,1,0:T(8,128)(2,1)S(1)}, u32[]{:S(2)}, u32[]{:S(2)}) collective-permute-start(bf16[4,8,2304]{2,1,0:T(8,128)(2,1)S(1)} %get-tuple-element.27), channel_id=1, source_target_pairs={{0,9},{1,8},{2,11},{3,10},{4,13},{5,12},{6,15},{7,14},{8,1},{9,0},... | collective-permute-start | bytes 442376 | tf_op jit(solution)/shard_map/ppermute | solution.py:199
  (25 other events, 224.0 us)
